TPU v7x, 128 devices: a whole 4x4x4 slice. The times are simulated.
128 devices in a mesh: tok: 16 (over x, y_lo, core), col: 8 (over y_hi, z).
Axes of the slice: x: 4, y: 4 (y_hi: 2, y_lo: 2; y = y_hi * 2 + y_lo), z: 4, core: 2. Of those that a mesh axis runs over, the one named last changes fastest.
Arguments:
- activations: bfloat16 [2, 24576, 4096], P(None, 'tok', 'col'), may hold values from -6 to 6
- out_grads: bfloat16 [2, 24576, 4096], P(None, 'tok', 'col'), may hold values from -0.059814453 to 0.059814453
- token_mask: int32 [2, 24576], P(None, 'tok'), may hold values 0 or 1
- row_signs: int32 [4096], P('tok'), may hold values from 0 to 1
- col_signs: int32 [4096], P('col'), may hold values from 0 to 1
- bank: float32 [16, 4096, 4096], P(None, 'tok', 'col'), may hold values from -6 to 6
- bank_index: int32 [2], replicated, may hold values from 0 to 15, as said below
Outputs:
- fingerprints: float32 [2, 4096, 4096], P(None, 'tok', 'col')
- scores: float32 [2], replicated
Inputs may be any that keep to these rules, and one draw needn't show every extreme that they name: `bank_index`: the 2 values are distinct, and one of them is 15.
All inputs are finite; a program needn't handle non-finite values. No bound on the sum of `token_mask` on one device may be relied on, other than what follows from the above.
Results may differ from a plain program's by a relative error of at most 0.0003.
Values may be sent and summed in bfloat16 or wider, within the bound.
A program may use at most 128 MiB of HBM per device.

v0:
```python
import functools
import math

import jax
import jax.numpy as jnp
from jax import lax
from jax.sharding import Mesh
from jax.sharding import PartitionSpec as P

D = 4096
TOK = ("tok_0", "tok_1", "tok_2")
COL = ("col_0", "col_1")
TOK_COL = ("tok_0", "tok_1", "tok_2", "col_0", "col_1")


HIGH = lax.Precision.HIGHEST


def copy_for_each(x, axis):
    peers = lax.axis_size(axis)
    return lax.all_to_all(jnp.broadcast_to(x[None], (peers, *x.shape)), axis, 0, 0, tiled=True)


def joined_along(pieces, dim):
    lengths = list(pieces.shape[1:])
    lengths[dim] *= pieces.shape[0]
    return jnp.moveaxis(pieces, 0, dim).reshape(lengths)


def gathered_copies(x, axis, dim):
    pieces = copy_for_each(x, axis)
    return joined_along(pieces, dim)


def one_axis_at_a_time(x, axes):
    return functools.reduce(lax.psum, axes, x)


def hadamard(order):
    positions = jnp.arange(order, dtype=jnp.int32)
    common_bits = jnp.bitwise_and(positions[:, None], positions[None, :])
    parity = jnp.zeros((order, order), jnp.int32)
    for bit_number in range(max(order.bit_length() - 1, 0)):
        parity = parity + jnp.bitwise_and(jnp.right_shift(common_bits, bit_number), 1)
    return (1 - 2 * (parity % 2)).astype(jnp.float32)


def body(activations, out_grads, token_mask, row_signs, col_signs, bank, bank_index):
    row_pm = (2 * row_signs - 1).astype(jnp.float32)
    col_pm = (2 * col_signs - 1).astype(jnp.float32)
    tok_count = lax.axis_size(TOK)
    col_count = lax.axis_size(COL)
    local_rows = row_pm.shape[0]
    local_cols = col_pm.shape[0]
    tok_table = hadamard(tok_count)
    col_table = hadamard(col_count)
    rows_table = hadamard(local_rows)
    cols_table = hadamard(local_cols)
    factor = 1.0 / math.sqrt(D)
    squared = float(D) * float(D)
    all_signs = gathered_copies(row_signs, TOK, 0)
    full_pm = (2 * all_signs - 1).astype(jnp.float32)
    prints = []
    crosses = []
    owns = []
    refsqs = []
    for seq_number in range(activations.shape[0]):
        features = lax.all_gather(activations[seq_number], COL, axis=1, tiled=True)
        masked = out_grads[seq_number] * token_mask[seq_number][:, None].astype(jnp.bfloat16)
        partial_value = jnp.einsum(
            "tr,tc->rc", features, masked, preferred_element_type=jnp.float32
        )
        blocks = (partial_value * full_pm[:, None]).reshape(tok_count, local_rows, local_cols)
        blocks = jnp.einsum("rs,asc->arc", rows_table, blocks, precision=HIGH)
        blocks = jnp.einsum("ab,brc->arc", tok_table, blocks, precision=HIGH)
        premixed = blocks.reshape(tok_count * local_rows, local_cols)

        def term_rows(row_start, row_count, premixed=premixed):
            return premixed

        summed = lax.psum_scatter(
            term_rows(jnp.int32(0), lax.axis_size(TOK) * local_rows),
            TOK,
            scatter_dimension=0,
            tiled=True,
        )
        slab = summed
        slab = slab * factor
        slab = jnp.dot(slab * col_pm[None, :], cols_table, precision=HIGH)
        pieces = slab.reshape(col_count, local_rows // col_count, local_cols)
        col_pieces = lax.all_to_all(pieces, COL, split_axis=0, concat_axis=0, tiled=True)
        mixed_cols = jnp.einsum("ab,brc->arc", col_table, col_pieces, precision=HIGH)
        pieces = lax.all_to_all(mixed_cols, COL, split_axis=0, concat_axis=0, tiled=True)
        slab = pieces.reshape(local_rows, local_cols)
        slab = slab * factor
        chosen = lax.dynamic_index_in_dim(bank, bank_index[seq_number], 0, keepdims=False)
        prints.append(slab)
        crosses.append(jnp.sum(slab * chosen))
        owns.append(jnp.sum(slab * slab))
        refsqs.append(jnp.sum(chosen * chosen))
    cross, own, refsq = (
        one_axis_at_a_time(jnp.stack(crosses), TOK_COL),
        one_axis_at_a_time(jnp.stack(owns), TOK_COL),
        one_axis_at_a_time(jnp.stack(refsqs), TOK_COL),
    )
    scores = D * (cross / squared) / jnp.sqrt((own / squared + 1e-06) * (refsq / squared + 1e-06))
    return (jnp.stack(prints), scores)


def solution(mesh):
    split = Mesh(mesh.devices.reshape(4, 2, 2, 2, 4), ("tok_0", "tok_1", "tok_2", "col_0", "col_1"))
    return jax.shard_map(
        body,
        mesh=split,
        in_specs=(
            P(None, TOK, COL),
            P(None, TOK, COL),
            P(None, TOK),
            P(TOK),
            P(COL),
            P(None, TOK, COL),
            P(),
        ),
        out_specs=(P(None, TOK, COL), P()),
        check_vma=False,
    )
```

profile of v0, /device:TPU:1, one launch (start us, length us, event | category | flops | bytes accessed | tf_op | source)
XLA Modules:
  0.0 615.3 jit_solution(9460281022073052252)
XLA Ops:
  7.2 0.0 copy-start.3
  7.2 0.0 copy-start
  7.2 0.0 copy-start.4
  7.2 0.0 all-gather.7.cloned.1.call-start
  7.2 4.0 fusion.135
  11.2 0.0 all-gather.7.cloned.1.call-update
  11.2 0.0 all-gather.5.cloned.1.call-start
  11.3 0.7 all-gather.5.cloned.1.call-update
  12.0 0.0 copy-done.3
  12.0 0.6 broadcast_in_dim.2
  12.6 6.8 %all-to-all-start = ((s32[16,1,256]{2,1,0:T(1,128)}), s32[16,1,256]{2,1,0:T(1,128)S(1)}, u32[]{:S(2)}, u32[]{:S(2)}) async-start(s32[16,1,256]{2,1,0:T(1,128)} %broadcast_in_dim.2), calls=%async_computation | async-start | bytes 32768 | tf_op jit(solution)/shard_map/all_to_all | solution.py:21
  19.4 0.0 reduce-scatter.5.cloned.1.call-start
  19.5 0.0 copy-done
  19.5 5.7 all-to-all-done
  25.3 141.2 %all-gather.7.cloned.1.call-done = bf16[1,1536,4096]{2,1,0:T(8,128)(2,1)} async-done(((bf16[1,1536,512]{2,1,0:T(8,128)(2,1)}), bf16[1,1536,4096]{2,1,0:T(8,128)(2,1)}) %all-gather.7.cloned.1.call-update) | async-done | bytes 12582928 | tf_op jit(solution)/shard_map/all_gather | solution.py:68
  166.5 0.0 copy-done.4
  166.5 10.4 %fusion.7 = f32[512,4096]{1,0:T(8,128)S(1)} fusion(bf16[1,1536,4096]{2,1,0:T(8,128)(2,1)} %all-gather.7.cloned.1.call-done, f32[4096]{0:T(1024)S(1)} %bitcast.87, bf16[2,1536,512]{2,1,0:T(8,128)(2,1)S(1)} %copy-done.4, bf16[1536]{0:T(1024)(128)(2,1)S(1)} %get-tuple-element.7), kind=kOutput, calls=%fused_computation.5 | convolution fusion | flops 6445334528 | bytes 22564864 | tf_op jit(solution)/shard_map/tr,tc->rc/dot_general | solution.py:70
  176.9 3.9 copy.28
  180.8 9.6 %convolution_bitcast_fusion = f32[16,256,512]{1,0,2:T(8,128)} fusion(f32[16,256,512]{1,0,2:T(8,128)S(1)} %bitcast.81), kind=kOutput, calls=%fused_computation.6 | convolution fusion | flops 6444941312 | bytes 16777216 | tf_op jit(solution)/shard_map/rs,asc->arc/dot_general | solution.py:74
  190.3 10.5 %copy.23 = f32[16,256,512]{2,0,1:T(8,128)} copy(f32[16,256,512]{1,0,2:T(8,128)} %convolution_bitcast_fusion) | data formatting | bytes 16777216 | tf_op jit(solution)/shard_map/rs,asc->arc/transpose | solution.py:74
  200.8 11.9 %fusion.62 = f32[16,256,512]{2,0,1:T(8,128)S(1)} fusion(f32[16,256,512]{2,0,1:T(8,128)} %copy.23), kind=kOutput, calls=%fused_computation.77 | convolution fusion | flops 402659840 | bytes 16777216 | tf_op jit(solution)/shard_map/ab,brc->arc/dot_general | solution.py:75
  212.7 8.0 %copy.24 = f32[16,256,512]{2,1,0:T(8,128)} copy(f32[16,256,512]{2,0,1:T(8,128)S(1)} %fusion.62) | data formatting | bytes 16777216 | tf_op jit(solution)/shard_map/ab,brc->arc/dot_general | solution.py:75
  220.8 0.0 reduce-scatter.5.cloned.1.call-update
  220.8 0.0 reduce-scatter.3.cloned.1.call-start
  220.9 98.2 %all-gather.5.cloned.1.call-done = bf16[1,1536,4096]{2,1,0:T(8,128)(2,1)} async-done(((bf16[1,1536,512]{2,1,0:T(8,128)(2,1)}), bf16[1,1536,4096]{2,1,0:T(8,128)(2,1)}) %all-gather.5.cloned.1.call-update) | async-done | bytes 12582928 | tf_op jit(solution)/shard_map/all_gather | solution.py:68
  319.1 10.5 %fusion.4 = f32[512,4096]{1,0:T(8,128)S(1)} fusion(bf16[1,1536,4096]{2,1,0:T(8,128)(2,1)} %all-gather.5.cloned.1.call-done, f32[4096]{0:T(1024)S(1)} %bitcast.88, bf16[2,1536,512]{2,1,0:T(8,128)(2,1)S(1)} %copy-done.4, bf16[1536]{0:T(1024)(128)(2,1)S(1)} %get-tuple-element.6), kind=kOutput, calls=%fused_computation.4 | convolution fusion | flops 6445334528 | bytes 22564864 | tf_op jit(solution)/shard_map/tr,tc->rc/dot_general | solution.py:70
  329.6 3.9 copy.27
  333.5 9.6 %convolution_bitcast_fusion.1 = f32[16,256,512]{1,0,2:T(8,128)} fusion(f32[16,256,512]{1,0,2:T(8,128)S(1)} %bitcast.82), kind=kOutput, calls=%fused_computation.7 | convolution fusion | flops 6444941312 | bytes 16777216 | tf_op jit(solution)/shard_map/rs,asc->arc/dot_general | solution.py:74
  343.1 10.5 %copy.19 = f32[16,256,512]{2,0,1:T(8,128)} copy(f32[16,256,512]{1,0,2:T(8,128)} %convolution_bitcast_fusion.1) | data formatting | bytes 16777216 | tf_op jit(solution)/shard_map/rs,asc->arc/transpose | solution.py:74
  353.6 11.6 %fusion.64 = f32[16,256,512]{2,0,1:T(8,128)S(1)} fusion(f32[16,256,512]{2,0,1:T(8,128)} %copy.19), kind=kOutput, calls=%fused_computation.78 | convolution fusion | flops 402659840 | bytes 16777216 | tf_op jit(solution)/shard_map/ab,brc->arc/dot_general | solution.py:75
  365.2 8.1 %copy.20 = f32[16,256,512]{2,1,0:T(8,128)} copy(f32[16,256,512]{2,0,1:T(8,128)S(1)} %fusion.64) | data formatting | bytes 16777216 | tf_op jit(solution)/shard_map/ab,brc->arc/dot_general | solution.py:75
  373.3 0.0 copy-start.1
  373.3 0.0 reduce-scatter.3.cloned.1.call-update
  373.3 0.7 copy-done.1
  374.0 42.7 %reduce-scatter.5.cloned.1.call-done = f32[256,512]{1,0:T(8,128)} async-done(((f32[4096,512]{1,0:T(8,128)}), f32[256,512]{1,0:T(8,128)}) %reduce-scatter.5.cloned.1.call-update) | async-done | bytes 524304 | tf_op jit(solution)/shard_map/reduce_scatter | solution.py:81
  416.7 4.3 fusion.26
  421.0 6.2 %all-to-all-start.3 = ((f32[8,32,512]{2,1,0:T(8,128)}), f32[8,32,512]{2,1,0:T(8,128)S(1)}, u32[]{:S(2)}, u32[]{:S(2)}) async-start(f32[8,32,512]{2,1,0:T(8,128)} %bitcast.16), calls=%async_computation.5 | async-start | bytes 1048576 | tf_op jit(solution)/shard_map/all_to_all | solution.py:91
  427.2 93.3 %reduce-scatter.3.cloned.1.call-done = f32[256,512]{1,0:T(8,128)} async-done(((f32[4096,512]{1,0:T(8,128)}), f32[256,512]{1,0:T(8,128)}) %reduce-scatter.3.cloned.1.call-update) | async-done | bytes 524304 | tf_op jit(solution)/shard_map/reduce_scatter | solution.py:81
  520.5 4.3 fusion.29
  524.8 0.0 all-to-all-done.3
  524.8 5.6 all-to-all-start.1
  530.4 0.8 fusion.22
  531.2 1.1 copy.26
  532.3 8.3 %all-to-all-done.1 = f32[8,32,512]{2,1,0:T(8,128)S(1)} async-done(((f32[8,32,512]{2,1,0:T(8,128)}), f32[8,32,512]{2,1,0:T(8,128)S(1)}, u32[]{:S(2)}, u32[]{:S(2)}) %all-to-all-start.1) | async-done | bytes 524320 | tf_op jit(solution)/shard_map/all_to_all | solution.py:91
  540.6 3.5 all-to-all-start.4
  544.1 0.8 fusion.24
  544.9 1.1 copy.22
  546.0 7.7 %all-to-all-done.4 = f32[8,32,512]{2,1,0:T(8,128)S(1)} async-done(((f32[8,32,512]{2,1,0:T(8,128)}), f32[8,32,512]{2,1,0:T(8,128)S(1)}, u32[]{:S(2)}, u32[]{:S(2)}) %all-to-all-start.4) | async-done | bytes 524320 | tf_op jit(solution)/shard_map/all_to_all | solution.py:93
  553.7 4.8 all-to-all-start.2
  558.5 0.0 copy-done.2
  558.5 0.6 fusion.136
  563.0 0.7 multiply_reduce_fusion
  563.7 4.0 all-to-all-done.2
  567.7 0.8 multiply_reduce_fusion.1
  568.5 1.0 pad_maximum_fusion
  569.6 2.0 fusion.20
  571.6 1.3 pad_maximum_fusion.3
  572.9 2.6 pad_maximum_fusion.1
  575.5 8.1 %all-reduce.1 = (f32[2]{0:T(128)S(1)}, f32[2]{0:T(128)S(1)}, f32[2]{0:T(128)S(1)}) all-reduce(f32[2]{0:T(128)S(1)} %pad_maximum_fusion.3, f32[2]{0:T(128)S(1)} %get-tuple-element.32, f32[2]{0:T(128)S(1)} %get-tuple-element.31), channel_id=1, replica_groups=mesh['tok_0'=4,'tok_1'=2,'tok_2'=2,'col_0'=2,'col_1'=4] {'tok_0'}, use_global_device_ids=true, to_apply=%region_18.19 | all-reduce | flops 6 | bytes 48 | tf_op jit(solution)/shard_map/psum | solution.py:36
  583.6 4.1 all-reduce.4
  587.7 7.7 %all-reduce.3 = (f32[2]{0:T(128)S(1)}, f32[2]{0:T(128)S(1)}, f32[2]{0:T(128)S(1)}) all-reduce(f32[2]{0:T(128)S(1)} %get-tuple-element.20, f32[2]{0:T(128)S(1)} %get-tuple-element.21, f32[2]{0:T(128)S(1)} %get-tuple-element.22), channel_id=1, replica_groups=mesh['tok_0'=4,'tok_1'=2,'tok_2'=2,'col_0'=2,'col_1'=4] {'tok_2'}, use_global_device_ids=true, to_apply=%region_20.21 | all-reduce | flops 6 | bytes 48 | tf_op jit(solution)/shard_map/psum | solution.py:36
  595.3 5.3 all-reduce.2
  600.6 7.2 %all-reduce = (f32[2]{0:T(128)S(1)}, f32[2]{0:T(128)S(1)}, f32[2]{0:T(128)S(1)}) all-reduce(f32[2]{0:T(128)S(1)} %get-tuple-element.14, f32[2]{0:T(128)S(1)} %get-tuple-element.15, f32[2]{0:T(128)S(1)} %get-tuple-element.16), channel_id=1, replica_groups=mesh['tok_0'=4,'tok_1'=2,'tok_2'=2,'col_0'=2,'col_1'=4] {'col_1'}, use_global_device_ids=true, to_apply=%region_22.23 | all-reduce | flops 6 | bytes 48 | tf_op jit(solution)/shard_map/psum | solution.py:36
  607.8 0.5 rsqrt_multiply_fusion
  (5 shorter events, 0.1 us)
Async XLA Ops:
  7.2 4.8 copy-start.3
  7.2 12.3 %copy-start = (s32[2,1536]{1,0:T(2,128)S(1)}, s32[2,1536]{1,0:T(2,128)}, u32[]{:S(2)}) copy-start(s32[2,1536]{1,0:T(2,128)} %param.9) | copy-start | bytes 36868
  7.2 159.3 %copy-start.4 = (bf16[2,1536,512]{2,1,0:T(8,128)(2,1)S(1)}, bf16[2,1536,512]{2,1,0:T(8,128)(2,1)}, u32[]{:S(2)}) copy-start(bf16[2,1536,512]{2,1,0:T(8,128)(2,1)} %param.8) | copy-start | bytes 9437188
  7.2 159.3 %all-gather.7.cloned.1.call-start = ((), (), s32[]{:S(2)}) async-start(), calls=%async_computation.10 | async-start | bytes 14155776 | tf_op jit(solution)/shard_map/all_gather | solution.py:68
  11.2 307.8 %all-gather.5.cloned.1.call-start = ((), (), s32[]{:S(2)}) async-start(), calls=%async_computation.9 | async-start | bytes 14155776 | tf_op jit(solution)/shard_map/all_gather | solution.py:68
  12.6 12.6 %all-to-all-start = ((s32[16,1,256]{2,1,0:T(1,128)}), s32[16,1,256]{2,1,0:T(1,128)S(1)}, u32[]{:S(2)}, u32[]{:S(2)}) async-start(s32[16,1,256]{2,1,0:T(1,128)} %broadcast_in_dim.2), calls=%async_computation | async-start | bytes 32768 | tf_op jit(solution)/shard_map/all_to_all | solution.py:21
  19.4 397.2 %reduce-scatter.5.cloned.1.call-start = ((), (), s32[]{:S(2)}) async-start(), calls=%async_computation.8 | async-start | bytes 8912896 | tf_op jit(solution)/shard_map/reduce_scatter | solution.py:81
  220.8 299.7 %reduce-scatter.3.cloned.1.call-start = ((), (), s32[]{:S(2)}) async-start(), calls=%async_computation.7 | async-start | bytes 8912896 | tf_op jit(solution)/shard_map/reduce_scatter | solution.py:81
  373.3 0.7 copy-start.1
  421.0 103.8 %all-to-all-start.3 = ((f32[8,32,512]{2,1,0:T(8,128)}), f32[8,32,512]{2,1,0:T(8,128)S(1)}, u32[]{:S(2)}, u32[]{:S(2)}) async-start(f32[8,32,512]{2,1,0:T(8,128)} %bitcast.16), calls=%async_computation.5 | async-start | bytes 1048576 | tf_op jit(solution)/shard_map/all_to_all | solution.py:91
  427.2 131.3 %copy-start.2 = (s32[2]{0:T(128)S(1)}, s32[2]{0:T(128)}, u32[]{:S(2)}) copy-start(s32[2]{0:T(128)} %param.13) | copy-start | bytes 28
  524.8 15.8 %all-to-all-start.1 = ((f32[8,32,512]{2,1,0:T(8,128)}), f32[8,32,512]{2,1,0:T(8,128)S(1)}, u32[]{:S(2)}, u32[]{:S(2)}) async-start(f32[8,32,512]{2,1,0:T(8,128)} %bitcast.9), calls=%async_computation.2 | async-start | bytes 1048576 | tf_op jit(solution)/shard_map/all_to_all | solution.py:91
  540.6 13.1 %all-to-all-start.4 = ((f32[8,32,512]{2,1,0:T(8,128)}), f32[8,32,512]{2,1,0:T(8,128)S(1)}, u32[]{:S(2)}, u32[]{:S(2)}) async-start(f32[8,32,512]{2,1,0:T(8,128)} %copy.26), calls=%async_computation.6 | async-start | bytes 1048576 | tf_op jit(solution)/shard_map/all_to_all | solution.py:93
  553.7 14.0 %all-to-all-start.2 = ((f32[8,32,512]{2,1,0:T(8,128)}), f32[8,32,512]{2,1,0:T(8,128)S(1)}, u32[]{:S(2)}, u32[]{:S(2)}) async-start(f32[8,32,512]{2,1,0:T(8,128)} %copy.22), calls=%async_computation.3 | async-start | bytes 1048576 | tf_op jit(solution)/shard_map/all_to_all | solution.py:93
Sparse Core Ops, SparseCore 0:
  11.4 155.0 all-gather.6
  168.7 150.3 all-gather.4
  321.5 95.1 reduce-scatter.4
  418.9 101.4 reduce-scatter.2
where the time goes:
time: 627 us; the launch traced here: 615 us
  waiting for transfers between devices  402 us (64%)
  matrix products  73.8 us (12%)
  local copies, waits for them, and re-layouts  53 us (8%)
  blocking collectives  32.3 us (5%)
  starting transfers between devices  27.1 us (4%)
  between operations  18.2 us (3%)
  other arithmetic  9.12 us (1%)
    all_gather x2, waiting for transfers between devices, body(): features = lax.all_gather(activations[seq_number], COL, axis=1, tiled=True)  239 us
    reduce_scatter x2, waiting for transfers between devices, body(): lax.psum_scatter(term_rows(jnp.int32(0), lax.axis_size(TOK) * local_rows)...  136 us
    psum x5, blocking collectives, one_axis_at_a_time(): return functools.reduce(lax.psum, axes, x)  32.3 us
    dot_general x2, matrix products, body(): blocks = jnp.einsum('ab,brc->arc', tok_table, blocks, precision=HIGH)  23.5 us
    transpose x2, local copies, waits for them, and re-layouts, body(): blocks = jnp.einsum('rs,asc->arc', rows_table, blocks, precision=HIGH)  21 us
    dot_general x2, matrix products, body(): jnp.einsum('tr,tc->rc', features, masked, preferred_element_type=jnp.floa...  20.9 us
    dot_general x2, matrix products, body(): blocks = jnp.einsum('rs,asc->arc', rows_table, blocks, precision=HIGH)  19.2 us
    dot_general x2, local copies, waits for them, and re-layouts, body(): blocks = jnp.einsum('ab,brc->arc', tok_table, blocks, precision=HIGH)  16.1 us
  transfers between devices with their start and end apart: 9, of which 8 were waited for; matrix products, arithmetic and copies ran while one was open for 20% of the time, Pallas kernels for 0%

commit v1 on v0

v1 whole, which is shorter than its diff:
```python
import functools
import math

import jax
import jax.numpy as jnp
from jax import lax
from jax.experimental import pallas as pl
from jax.experimental.pallas import tpu as pltpu
from jax.sharding import Mesh
from jax.sharding import PartitionSpec as P

D = 4096
TOK = ("tok_0", "tok_1", "tok_2")
COL = ("col_0", "col_1")
EVERY = ("tok_0", "tok_1", "tok_2", "col_0", "col_1")
HIGH = lax.Precision.HIGHEST
MESH = pl.DeviceIdType.MESH

SEQS = 2
TOKENS = 1536
HALF = TOKENS // 2
FEATS = 512
BLOCKS = 4
UNITS = SEQS * BLOCKS


def hadamard(order):
    positions = jnp.arange(order, dtype=jnp.int32)
    common_bits = jnp.bitwise_and(positions[:, None], positions[None, :])
    parity = jnp.zeros((order, order), jnp.int32)
    for bit_number in range(max(order.bit_length() - 1, 0)):
        parity = parity + jnp.bitwise_and(jnp.right_shift(common_bits, bit_number), 1)
    return (1 - 2 * (parity % 2)).astype(jnp.float32)


def gather_kernel(
    acts,
    grads,
    tables,
    out,
    a_buf,
    m_buf,
    relay,
    turned,
    part,
    core_in,
    x_half,
    x_full,
    y_in,
    load_sem,
    a_send,
    a_recv,
    m_send,
    m_recv,
    core_send,
    core_recv,
    xh_send,
    xh_recv,
    xf_send,
    xf_recv,
    y_send,
    y_recv,
):
    x = lax.axis_index("tok_0")
    y_lo = lax.axis_index("tok_1")
    core = lax.axis_index("tok_2")
    y_hi = lax.axis_index("col_0")
    z = lax.axis_index("col_1")
    y = y_hi * 2 + y_lo

    def at_y(value):
        value = lax.rem(value, 4)
        return (x, lax.rem(value, 2), core, lax.div(value, 2), z)

    x_next, x_prev, x_far = lax.rem(x + 1, 4), lax.rem(x + 3, 4), lax.rem(x + 2, 4)
    z_ids = ((x, y_lo, core, y_hi, lax.rem(z + 1, 4)), (x, y_lo, core, y_hi, lax.rem(z + 3, 4)))
    y_ids = (at_y(y + 1), at_y(y + 3))
    x_ids = ((x_next, y_lo, core, y_hi, z), (x_prev, y_lo, core, y_hi, z))
    core_id = (x, y_lo, 1 - core, y_hi, z)
    pair_id = (x, 1 - y_lo, core, y_hi, z)

    loads = []
    for seq in range(SEQS):
        loads.append(pltpu.make_async_copy(acts.at[seq], a_buf.at[seq, 0], load_sem.at[2 * seq]))
        loads.append(pltpu.make_async_copy(grads.at[seq], m_buf.at[seq, 0], load_sem.at[2 * seq + 1]))
    for copy in loads:
        copy.start()

    barrier = pltpu.get_barrier_semaphore()
    partners = (*z_ids, *y_ids, *x_ids, core_id)
    for partner in partners:
        pl.semaphore_signal(barrier, inc=1, device_id=partner, device_id_type=MESH)
    pl.semaphore_wait(barrier, len(partners))

    def rows_of(half):
        return pl.ds(half * HALF, HALF)

    def remote(src, dst, send, recv, device):
        return pltpu.make_async_remote_copy(
            src_ref=src, dst_ref=dst, send_sem=send, recv_sem=recv, device_id=device, device_id_type=MESH
        )

    def ring_copy(seq, way, half, hop):
        slot = (3, 1)[way] if hop == 0 else 2
        index = (seq * 2 + way) * 3 + (2 if hop else half)
        src = acts.at[seq, rows_of(half)] if hop == 0 else a_buf.at[seq, (3, 1)[way], rows_of(half)]
        return remote(src, a_buf.at[seq, slot, rows_of(half)], a_send.at[index], a_recv.at[index], z_ids[way])

    def swap_copy(seq, way, hop):
        index = (seq * 2 + way) * 2 + hop
        src = relay.at[seq, way] if hop else grads.at[seq, rows_of(way)]
        dst = m_buf.at[seq, 1, rows_of(way)] if hop else relay.at[seq, way]
        return remote(src, dst, m_send.at[index], m_recv.at[index], y_ids[way])

    sent = []

    def start(copy):
        copy.start()
        sent.append(copy)

    def ring_own(seq):
        for step in range(2):
            for way in range(2):
                start(ring_copy(seq, way, (way + step) % 2, 0))

    def ring_pass(seq):
        for way in range(2):
            ring_copy(seq, way, way, 0).wait_recv()
            start(ring_copy(seq, way, way, 1))

    def swap_own(seq):
        for way in range(2):
            start(swap_copy(seq, way, 0))

    def swap_pass(seq):
        for way in range(2):
            swap_copy(seq, way, 0).wait_recv()
            start(swap_copy(seq, way, 1))

    def swap_end(seq):
        for way in range(2):
            swap_copy(seq, way, 1).wait_recv()

    def ring_near(seq, way):
        ring_copy(seq, way, 1 - way, 0).wait_recv()

    def ring_far(seq):
        for way in range(2):
            ring_copy(seq, way, way, 1).wait_recv()

    core_sign = (1 - 2 * core).astype(jnp.float32)

    def compute(unit, seq, slot):
        block = lax.rem(z + slot, 4)

        @pl.loop(0, 2)
        def _(b):
            columns = pl.ds(pl.multiple_of(b * 256, 256), 256)
            turned[b] = a_buf[seq, slot, :, columns].T

        @pl.loop(0, 4)
        def _(i):
            b = lax.div(i, 2)
            m = lax.rem(i, 2)
            tile = jnp.dot(turned[b], m_buf[seq, m], preferred_element_type=jnp.float32)
            coarse = tile.astype(jnp.bfloat16)
            fine = (tile - coarse.astype(jnp.float32)).astype(jnp.bfloat16)
            table = tables[2 * block + b]
            mixed = jnp.dot(table, coarse, preferred_element_type=jnp.float32)
            mixed += jnp.dot(table, fine, preferred_element_type=jnp.float32)
            columns = pl.ds(pl.multiple_of(lax.rem(m + y_hi, 2) * 512, 512), 512)
            part[unit, b, :, columns] = mixed

        @pl.loop(0, 32)
        def _(i):
            rows = pl.ds(pl.multiple_of(i * 8, 8), 8)
            low = part[unit, 0, rows]
            high = part[unit, 1, rows] * core_sign
            part[unit, 0, rows] = low + high
            part[unit, 1, rows] = low - high

        start(core_copy(unit))

    def core_copy(unit):
        return remote(part.at[unit, 1], core_in.at[unit], core_send.at[unit], core_recv.at[unit], core_id)

    def chunk(unit, x_of):
        return part.at[unit, 0, pl.ds(pl.multiple_of(x_of * 64, 64), 64)]

    def x_half_copy(unit, way):
        rows = pl.ds(pl.multiple_of(x_far * 64 + way * 32, 32), 32)
        index = unit * 2 + way
        return remote(
            part.at[unit, 0, rows], x_half.at[unit, way], xh_send.at[index], xh_recv.at[index], x_ids[way]
        )

    def x_full_copy(unit, way):
        index = unit * 2 + way
        src = chunk(unit, (x_next, x_prev)[way])
        return remote(src, x_full.at[unit, way], xf_send.at[index], xf_recv.at[index], x_ids[way])

    def y_copy(unit):
        rows = pl.ds(pl.multiple_of(x * 64 + (1 - y_lo) * 32, 32), 32)
        return remote(part.at[unit, 0, rows], y_in.at[unit], y_send.at[unit], y_recv.at[unit], pair_id)

    def sum_core(unit):
        core_copy(unit).wait_recv()

        def add(first, rows):
            @pl.loop(0, rows // 8)
            def _(i):
                there = pl.ds(pl.multiple_of(first + i * 8, 8), 8)
                part[unit, 0, there] += core_in[unit, there]

        add(x_far * 64, 64)
        for way in range(2):
            start(x_half_copy(unit, way))
        for other in (x_next, x_prev, x):
            add(other * 64, 64)

    def sum_half(unit):
        for way in range(2):
            x_half_copy(unit, way).wait_recv()
            first = (x_next, x_prev)[way] * 64 + way * 32

            @pl.loop(0, 4)
            def _(i):
                there = pl.ds(pl.multiple_of(first + i * 8, 8), 8)
                part[unit, 0, there] += x_half[unit, way, pl.ds(pl.multiple_of(i * 8, 8), 8)]

            start(x_full_copy(unit, way))

    def sum_full(unit):
        for way in range(2):
            x_full_copy(unit, way).wait_recv()

        @pl.loop(0, 8)
        def _(i):
            there = pl.ds(pl.multiple_of(x * 64 + i * 8, 8), 8)
            here = pl.ds(pl.multiple_of(i * 8, 8), 8)
            part[unit, 0, there] += x_full[unit, 0, here] + x_full[unit, 1, here]

        start(y_copy(unit))

    def finish(unit, seq, slot):
        block = lax.rem(z + slot, 4)
        y_copy(unit).wait_recv()

        @pl.loop(0, 4)
        def _(i):
            here = pl.ds(pl.multiple_of(i * 8, 8), 8)
            there = pl.ds(pl.multiple_of(x * 64 + y_lo * 32 + i * 8, 8), 8)
            out[seq, block, here] = part[unit, 0, there] + y_in[unit, here]

    order = [(seq, slot) for seq in range(SEQS) for slot in (0, 3, 1, 2)]
    run = [functools.partial(compute, unit, *order[unit]) for unit in range(UNITS)]
    end = [functools.partial(finish, unit, *order[unit]) for unit in range(UNITS)]

    ring_own(0)
    swap_own(0)
    swap_pass(0)
    swap_own(1)
    ring_pass(0)
    ring_own(1)
    for copy in loads:
        copy.wait()
    swap_end(0)
    run[0]()
    ring_near(0, 0)
    run[1]()
    sum_core(0)
    ring_near(0, 1)
    run[2]()
    sum_core(1)
    sum_half(0)
    sum_core(2)
    sum_half(1)
    swap_pass(1)
    sum_full(0)
    sum_half(2)
    ring_far(0)
    run[3]()
    sum_core(3)
    sum_full(1)
    end[0]()
    sum_half(3)
    sum_full(2)
    end[1]()
    ring_pass(1)
    swap_end(1)
    run[4]()
    sum_core(4)
    sum_full(3)
    end[2]()
    sum_half(4)
    end[3]()
    sum_full(4)
    ring_near(1, 0)
    run[5]()
    ring_near(1, 1)
    run[6]()
    sum_core(5)
    sum_core(6)
    sum_half(5)
    sum_half(6)
    end[4]()
    sum_full(5)
    sum_full(6)
    ring_far(1)
    run[7]()
    sum_core(7)
    end[5]()
    end[6]()
    sum_half(7)
    sum_full(7)
    end[7]()
    for copy in sent:
        copy.wait_send()


def gathered_products(acts, grads, tables):
    dma = pltpu.SemaphoreType.DMA
    return pl.pallas_call(
        gather_kernel,
        out_shape=jax.ShapeDtypeStruct((SEQS, BLOCKS, 32, 2 * FEATS), jnp.float32),
        in_specs=[
            pl.BlockSpec(memory_space=pl.ANY),
            pl.BlockSpec(memory_space=pl.ANY),
            pl.BlockSpec(memory_space=pltpu.VMEM),
        ],
        out_specs=pl.BlockSpec(memory_space=pltpu.VMEM),
        scratch_shapes=[
            pltpu.VMEM((SEQS, BLOCKS, TOKENS, FEATS), jnp.bfloat16),
            pltpu.VMEM((SEQS, 2, TOKENS, FEATS), jnp.bfloat16),
            pltpu.VMEM((SEQS, 2, HALF, FEATS), jnp.bfloat16),
            pltpu.VMEM((2, 256, TOKENS), jnp.bfloat16),
            pltpu.VMEM((UNITS, 2, 256, 2 * FEATS), jnp.float32),
            pltpu.VMEM((UNITS, 256, 2 * FEATS), jnp.float32),
            pltpu.VMEM((UNITS, 2, 32, 2 * FEATS), jnp.float32),
            pltpu.VMEM((UNITS, 2, 64, 2 * FEATS), jnp.float32),
            pltpu.VMEM((UNITS, 32, 2 * FEATS), jnp.float32),
            dma((4,)),
            dma((12,)),
            dma((12,)),
            dma((8,)),
            dma((8,)),
            dma((UNITS,)),
            dma((UNITS,)),
            dma((2 * UNITS,)),
            dma((2 * UNITS,)),
            dma((2 * UNITS,)),
            dma((2 * UNITS,)),
            dma((UNITS,)),
            dma((UNITS,)),
        ],
        compiler_params=pltpu.CompilerParams(
            collective_id=0, has_side_effects=True, vmem_limit_bytes=67043328
        ),
    )(acts, grads, tables)


def body(activations, out_grads, token_mask, row_signs, col_signs, bank, bank_index):
    squared = float(D) * float(D)
    y_hi = lax.axis_index("col_0")
    all_signs = lax.all_gather(row_signs, TOK, axis=0, tiled=True)
    mine = lax.dynamic_slice_in_dim(all_signs, y_hi * 2048, 2048, 0)
    signs = (2 * mine - 1).astype(jnp.float32).reshape(8, 1, 256)
    tables = (hadamard(256)[None] * signs).astype(jnp.bfloat16)
    col_pm = (2 * col_signs - 1).astype(jnp.bfloat16)
    grads = out_grads * token_mask[:, :, None].astype(jnp.bfloat16) * col_pm[None, None, :]

    sums = gathered_products(activations, grads, tables)

    sums = jnp.einsum("am,sapc->smpc", hadamard(4), sums, precision=HIGH)
    sums = sums.reshape(SEQS, 4, 32, 2, 512)
    sums = jnp.einsum("yh,smpyc->smphc", hadamard(2), sums, precision=HIGH)
    sums = jnp.dot(sums, hadamard(512), precision=HIGH) * (1.0 / D)
    pieces = sums.reshape(SEQS, 4, 4, 8, 2, 512).transpose(4, 2, 0, 1, 3, 5).reshape(8, SEQS, 4, 8, 512)
    pieces = lax.all_to_all(pieces, COL, split_axis=0, concat_axis=0, tiled=True)
    pieces = jnp.einsum("ab,bsmpc->asmpc", hadamard(8), pieces, precision=HIGH)
    pieces = pieces.reshape(2, 4, SEQS, 4, 8, 512).transpose(0, 3, 1, 2, 4, 5).reshape(32, SEQS, 8, 512)
    pieces = lax.all_to_all(pieces, ("tok_0", "tok_1", "col_1"), split_axis=0, concat_axis=0, tiled=True)
    prints = pieces.transpose(1, 0, 2, 3).reshape(SEQS, 256, 512)

    chosen = jnp.stack(
        [lax.dynamic_index_in_dim(bank, bank_index[seq], 0, keepdims=False) for seq in range(SEQS)]
    )
    totals = jnp.concatenate(
        [
            jnp.sum(prints * chosen, axis=(1, 2)),
            jnp.sum(prints * prints, axis=(1, 2)),
            jnp.sum(chosen * chosen, axis=(1, 2)),
        ]
    )
    totals = lax.psum(totals, EVERY)
    cross, own, refsq = totals[0:2], totals[2:4], totals[4:6]
    scores = D * (cross / squared) / jnp.sqrt((own / squared + 1e-06) * (refsq / squared + 1e-06))
    return prints, scores


def solution(mesh):
    split = Mesh(mesh.devices.reshape(4, 2, 2, 2, 4), EVERY)
    return jax.shard_map(
        body,
        mesh=split,
        in_specs=(
            P(None, TOK, COL),
            P(None, TOK, COL),
            P(None, TOK),
            P(TOK),
            P(COL),
            P(None, TOK, COL),
            P(),
        ),
        out_specs=(P(None, TOK, COL), P()),
        check_vma=False,
    )
```

time: 627 us -> 306 us (0.49); the launches traced: 615 us -> 305 us
  waiting for transfers between devices: 402 us -> 6.78 us
  Pallas kernels: 0 us -> 158 us
  blocking collectives: 32.3 us -> 104 us
  matrix products: 73.8 us -> 12.6 us
  local copies, waits for them, and re-layouts: 53 us -> 6.04 us
  starting transfers between devices: 27.1 us -> 5.44 us
  between operations: 18.2 us -> 4.75 us
    all_gather x2 -> x0, waiting for transfers between devices: 239 us -> none  [body(): features = lax.all_gather(activations[seq_number], COL, axis=1, tiled=True)]
    pallas_call x0 -> x1, Pallas kernels: none -> 158 us  [gathered_products(): pl.pallas_call(gather_kernel, out_shape=jax.ShapeDtypeStruct((SEQS, BLOCK...]
    reduce_scatter x2 -> x0, waiting for transfers between devices: 136 us -> none  [body(): lax.psum_scatter(term_rows(jnp.int32(0), lax.axis_size(TOK) * local_rows)...]
    dot_general x10 -> x4, matrix products: 73.8 us -> 12.6 us  [the longest x1 4.01 us: body(): sums = jnp.einsum('yh,smpyc->smphc', hadamard(2), sums, precision=HIGH)]
    psum x5 -> x1, blocking collectives: 32.3 us -> 66.2 us  [body(): totals = lax.psum(totals, EVERY)]
    all_to_all x5 -> x1, starting transfers between devices: 26.9 us -> 5.44 us  [body(): lax.all_to_all(pieces, ('tok_0', 'tok_1', 'col_1'), split_axis=0, concat_...]
    all_gather x0 -> x1, blocking collectives: none -> 21.3 us  [body(): all_signs = lax.all_gather(row_signs, TOK, axis=0, tiled=True)]
    transpose x2 -> x1, local copies, waits for them, and re-layouts: 21 us -> 0.08 us  [body(): sums.reshape(SEQS, 4, 4, 8, 2, 512).transpose(4, 2, 0, 1, 3, 5)]
  transfers between devices with their start and end apart: 9 -> 1, of which waited for: 8 -> 1; matrix products, arithmetic and copies ran while one was open for 20% -> 1% of each run, Pallas kernels for 0% -> 0%
where the time goes in v1:
time: 306 us; the launch traced here: 305 us
  Pallas kernels  158 us (52%)
  blocking collectives  104 us (34%)
  matrix products  12.6 us (4%)
  other arithmetic  7.62 us (2%)
  waiting for transfers between devices  6.78 us (2%)
  local copies, waits for them, and re-layouts  6.04 us (2%)
  starting transfers between devices  5.44 us (2%)
  between operations  4.75 us (2%)
    pallas_call x1, Pallas kernels, gathered_products(): pl.pallas_call(gather_kernel, out_shape=jax.ShapeDtypeStruct((SEQS, BLOCK...  158 us
    psum x1, blocking collectives, body(): totals = lax.psum(totals, EVERY)  66.2 us
    all_gather x1, blocking collectives, body(): all_signs = lax.all_gather(row_signs, TOK, axis=0, tiled=True)  21.3 us
    all_to_all x1, blocking collectives, body(): lax.all_to_all(pieces, COL, split_axis=0, concat_axis=0, tiled=True)  16.9 us
    all_to_all x1, waiting for transfers between devices, body(): lax.all_to_all(pieces, ('tok_0', 'tok_1', 'col_1'), split_axis=0, concat_...  6.78 us
  transfers between devices with their start and end apart: 1, of which 1 were waited for; matrix products, arithmetic and copies ran while one was open for 1% of the time, Pallas kernels for 0%

profile of v1, /device:TPU:1, one launch (start us, length us, event | category | flops | bytes accessed | tf_op | source)
XLA Modules:
  0.0 305.5 jit_solution(11272134116268418912)
XLA Ops:
  0.6 0.3 fusion.29
  1.0 0.7 add_convert_fusion.1
  1.7 0.7 convert_element_type.33
  2.4 21.3 %all-gather = s32[16,1,256]{2,1,0:T(1,128)S(1)} all-gather(s32[1,1,256]{2,1,0:T(1,128)} %bitcast.55), channel_id=1, replica_groups=mesh['tok_0'=4,'tok_1'=2,'tok_2'=2,'col_0'=2,'col_1'=4] {'tok_0','tok_1'..., dimensions={0}, use_global_device_ids=true | all-gather | bytes 17408 | tf_op jit(solution)/shard_map/all_gather | solution.py:365
  23.7 1.2 multiply_convert_fusion.tables
  24.9 3.3 %multiply_multiply_fusion.grads = bf16[2,1536,512]{2,1,0:T(8,128)(2,1)} fusion(bf16[2,1536,512]{2,1,0:T(8,128)(2,1)} %param.8, bf16[512]{0:T(512)(128)(2,1)S(1)} %add_convert_fusion.1, bf16[2,1536]{1,0:T(2,128)(2,1)S(1)} %convert_element_type.33), kind=kLoop, calls=%fused_computation | loop fusion | flops 3145728 | bytes 6298624 | tf_op jit(solution)/shard_map/mul | solution.py:370
  28.2 157.9 %shard_map.86 = f32[2,4,32,1024]{3,2,1,0:T(8,128)} custom-call(bf16[2,1536,512]{2,1,0:T(8,128)(2,1)} %acts.1, bf16[2,1536,512]{2,1,0:T(8,128)(2,1)} %multiply_multiply_fusion.grads, bf16[8,256,256]{2,1,0:T(8,128)(2,1)} %multiply_convert_fusion.tables), custom_call_target="tpu_custom_call" | custom-call | tf_op jit(solution)/shard_map/pallas_call | solution.py:323
  186.1 3.7 %convolution_bitcast_fusion.1 = f32[2,4,32,1024]{3,1,2,0:T(4,128)S(1)} fusion(f32[2,4,32,1024]{3,2,1,0:T(8,128)} %shard_map.86), kind=kOutput, calls=%fused_computation.8 | convolution fusion | flops 12583232 | bytes 2097152 | tf_op jit(solution)/shard_map/am,sapc->smpc/dot_general | solution.py:374
  189.8 1.1 reshape.78
  190.9 4.0 %convolution_bitcast_fusion = f32[2,4,32,2,512]{4,3,2,1,0:T(2,128)S(1)} fusion(f32[2,4,32,2,512]{4,3,1,2,0:T(2,128)S(1)} %reshape.78), kind=kOutput, calls=%fused_computation.5 | convolution fusion | flops 6291524 | bytes 2097152 | tf_op jit(solution)/shard_map/yh,smpyc->smphc/dot_general | solution.py:376
  194.9 3.4 %fusion = f32[2,4,2,4,8,512]{5,4,1,0,3,2:T(8,128)S(1)} fusion(f32[2,4,32,2,512]{4,3,2,1,0:T(2,128)S(1)} %convolution_bitcast_fusion), kind=kOutput, calls=%fused_computation.7 | convolution fusion | flops 1621622784 | bytes 2097152 | tf_op jit(solution)/shard_map/dot_general | solution.py:377
  198.3 0.1 copy.23
  198.4 16.9 %all_to_all.10 = f32[8,2,4,8,512]{4,3,2,1,0:T(8,128)S(1)} all-to-all(f32[8,2,4,8,512]{4,3,2,1,0:T(8,128)S(1)} %bitcast.53), channel_id=1, replica_groups=mesh['tok_0'=4,'tok_1'=2,'tok_2'=2,'col_0'=2,'col_1'=4] {'col_0','col_1'}, dimensions={0} | all-to-all | bytes 2097152 | tf_op jit(solution)/shard_map/all_to_all | solution.py:379
  215.3 1.5 fusion.9
  216.8 0.0 copy-start
  216.8 0.3 reshape.81
  217.1 1.6 copy.25
  218.7 5.4 %all-to-all-start.1 = ((f32[32,2,8,512]{3,2,1,0:T(8,128)}), f32[32,2,8,512]{3,2,1,0:T(8,128)S(1)}, u32[]{:S(2)}, u32[]{:S(2)}) async-start(f32[32,2,8,512]{3,2,1,0:T(8,128)} %bitcast.16), calls=%async_computation.1 | async-start | bytes 2097152 | tf_op jit(solution)/shard_map/all_to_all | solution.py:382
  224.1 0.0 copy-done
  224.2 0.7 fusion.86
  228.8 1.3 constant_dynamic-slice_fusion.1
  230.1 0.2 fusion.8
  230.3 6.8 %all-to-all-done.1 = f32[32,2,8,512]{3,2,1,0:T(8,128)S(1)} async-done(((f32[32,2,8,512]{3,2,1,0:T(8,128)}), f32[32,2,8,512]{3,2,1,0:T(8,128)S(1)}, u32[]{:S(2)}, u32[]{:S(2)}) %all-to-all-start.1) | async-done | bytes 1048608 | tf_op jit(solution)/shard_map/all_to_all | solution.py:382
  237.1 0.4 fusion.7
  237.5 0.1 pad_maximum_fusion
  237.6 66.2 %psum.7 = f32[6]{0:T(128)S(1)} all-reduce(f32[6]{0:T(128)S(1)} %pad_maximum_fusion), channel_id=1, replica_groups=mesh['tok_0'=4,'tok_1'=2,'tok_2'=2,'col_0'=2,'col_1'=4] {'tok_0','tok_1'..., use_global_device_ids=true, to_apply=%region_3.4 | all-reduce | flops 6 | bytes 48 | tf_op jit(solution)/shard_map/psum | solution.py:395
  303.8 0.6 rsqrt_multiply_fusion
  304.4 1.1 copy_bitcast_fusion
  (2 shorter events, 0.0 us)
Async XLA Ops:
  216.8 7.4 %copy-start = (s32[2]{0:T(128)S(1)}, s32[2]{0:T(128)}, u32[]{:S(2)}) copy-start(s32[2]{0:T(128)} %param.13) | copy-start | bytes 28
  218.7 18.4 %all-to-all-start.1 = ((f32[32,2,8,512]{3,2,1,0:T(8,128)}), f32[32,2,8,512]{3,2,1,0:T(8,128)S(1)}, u32[]{:S(2)}, u32[]{:S(2)}) async-start(f32[32,2,8,512]{3,2,1,0:T(8,128)} %bitcast.16), calls=%async_computation.1 | async-start | bytes 2097152 | tf_op jit(solution)/shard_map/all_to_all | solution.py:382

commit v2 on v1

--- a/solution.py
+++ b/solution.py
@@ -13,7 +13,6 @@
 TOK = ("tok_0", "tok_1", "tok_2")
 COL = ("col_0", "col_1")
 EVERY = ("tok_0", "tok_1", "tok_2", "col_0", "col_1")
-HIGH = lax.Precision.HIGHEST
 MESH = pl.DeviceIdType.MESH
 
 SEQS = 2
@@ -36,8 +35,11 @@
 def gather_kernel(
     acts,
     grads,
+    row_bits,
+    walsh,
+    out,
+    bits,
     tables,
-    out,
     a_buf,
     m_buf,
     relay,
@@ -60,6 +62,9 @@
     xf_recv,
     y_send,
     y_recv,
+    bit_load,
+    bit_send,
+    bit_recv,
 ):
     x = lax.axis_index("tok_0")
     y_lo = lax.axis_index("tok_1")
@@ -83,6 +88,7 @@
     for seq in range(SEQS):
         loads.append(pltpu.make_async_copy(acts.at[seq], a_buf.at[seq, 0], load_sem.at[2 * seq]))
         loads.append(pltpu.make_async_copy(grads.at[seq], m_buf.at[seq, 0], load_sem.at[2 * seq + 1]))
+    loads.append(pltpu.make_async_copy(row_bits, bits.at[y_lo, x, core], bit_load))
     for copy in loads:
         copy.start()
 
@@ -147,6 +153,30 @@
     def ring_far(seq):
         for way in range(2):
             ring_copy(seq, way, way, 1).wait_recv()
+
+    def bit_copy(index, ref, device):
+        return remote(ref, ref, bit_send.at[index], bit_recv.at[index], device)
+
+    def share_bits():
+        loads.pop().wait()
+        start(bit_copy(0, bits.at[y_lo, x, core], core_id))
+        bit_copy(0, bits.at[y_lo, x, core], core_id).wait_recv()
+        for way in range(2):
+            start(bit_copy(1 + way, bits.at[y_lo, x], x_ids[way]))
+        for way in range(2):
+            bit_copy(1 + way, bits.at[y_lo, x], x_ids[way]).wait_recv()
+        start(bit_copy(3, bits.at[y_lo, x_prev], x_ids[0]))
+        bit_copy(3, bits.at[y_lo, x_prev], x_ids[0]).wait_recv()
+        start(bit_copy(4, bits.at[y_lo], pair_id))
+
+    def sign_tables():
+        bit_copy(4, bits.at[y_lo], pair_id).wait_recv()
+
+        @pl.loop(0, 8)
+        def _(i):
+            row = bits[lax.rem(lax.div(i, 2), 2), 2 * y_hi + lax.div(i, 4), lax.rem(i, 2)]
+            signs = (2 * row - 1).astype(jnp.float32)
+            tables[i] = (walsh[...] * signs).astype(jnp.bfloat16)
 
     core_sign = (1 - 2 * core).astype(jnp.float32)
 
@@ -258,12 +288,14 @@
 
     ring_own(0)
     swap_own(0)
+    share_bits()
     swap_pass(0)
     swap_own(1)
     ring_pass(0)
     ring_own(1)
     for copy in loads:
         copy.wait()
+    sign_tables()
     swap_end(0)
     run[0]()
     ring_near(0, 0)
@@ -318,7 +350,7 @@
         copy.wait_send()
 
 
-def gathered_products(acts, grads, tables):
+def gathered_products(acts, grads, row_bits, walsh):
     dma = pltpu.SemaphoreType.DMA
     return pl.pallas_call(
         gather_kernel,
@@ -326,10 +358,13 @@
         in_specs=[
             pl.BlockSpec(memory_space=pl.ANY),
             pl.BlockSpec(memory_space=pl.ANY),
+            pl.BlockSpec(memory_space=pl.ANY),
             pl.BlockSpec(memory_space=pltpu.VMEM),
         ],
         out_specs=pl.BlockSpec(memory_space=pltpu.VMEM),
         scratch_shapes=[
+            pltpu.VMEM((2, 4, 2, 1, 256), jnp.int32),
+            pltpu.VMEM((8, 256, 256), jnp.bfloat16),
             pltpu.VMEM((SEQS, BLOCKS, TOKENS, FEATS), jnp.bfloat16),
             pltpu.VMEM((SEQS, 2, TOKENS, FEATS), jnp.bfloat16),
             pltpu.VMEM((SEQS, 2, HALF, FEATS), jnp.bfloat16),
@@ -352,48 +387,272 @@
             dma((2 * UNITS,)),
             dma((UNITS,)),
             dma((UNITS,)),
+            dma,
+            dma((5,)),
+            dma((5,)),
         ],
         compiler_params=pltpu.CompilerParams(
             collective_id=0, has_side_effects=True, vmem_limit_bytes=67043328
         ),
-    )(acts, grads, tables)
+    )(acts, grads, row_bits, walsh)
+
+
+def mix_kernel(
+    sums,
+    chosen,
+    walsh,
+    out,
+    totals,
+    work,
+    got,
+    ready,
+    land,
+    mine,
+    theirs,
+    late,
+    late_in,
+    col_send,
+    col_recv,
+    grp_send,
+    grp_recv,
+    red_send,
+    red_recv,
+    late_send,
+    late_recv,
+):
+    x = lax.axis_index("tok_0")
+    y_lo = lax.axis_index("tok_1")
+    core = lax.axis_index("tok_2")
+    y_hi = lax.axis_index("col_0")
+    z = lax.axis_index("col_1")
+    col_me = y_hi * 4 + z
+    grp_me = x * 8 + y_lo * 4 + z
+
+    def col_peer(j):
+        there_y = lax.rem(y_hi + lax.div(j, 4), 2)
+        there_z = lax.rem(z + j, 4)
+        return there_y * 4 + there_z, (x, y_lo, core, there_y, there_z)
+
+    def grp_peer(j):
+        there_x = lax.rem(x + lax.div(j, 8), 4)
+        there_y = lax.rem(y_lo + lax.div(j, 4), 2)
+        there_z = lax.rem(z + j, 4)
+        return there_x * 8 + there_y * 4 + there_z, (there_x, there_y, core, y_hi, there_z)
+
+    core_id = (x, y_lo, 1 - core, y_hi, z)
+    far_id = (x, y_lo, core, 1 - y_hi, z)
+
+    barrier = pltpu.get_barrier_semaphore()
+
+    @pl.loop(1, 8)
+    def _(j):
+        pl.semaphore_signal(barrier, inc=1, device_id=col_peer(j)[1], device_id_type=MESH)
+
+    @pl.loop(1, 32)
+    def _(j):
+        pl.semaphore_signal(barrier, inc=1, device_id=grp_peer(j)[1], device_id_type=MESH)
+
+    pl.semaphore_signal(barrier, inc=1, device_id=core_id, device_id_type=MESH)
+
+    def remote(src, dst, send, recv, device):
+        return pltpu.make_async_remote_copy(
+            src_ref=src, dst_ref=dst, send_sem=send, recv_sem=recv, device_id=device, device_id_type=MESH
+        )
+
+    def piece(peer):
+        return pl.ds(pl.multiple_of(peer * 32, 32), 32)
+
+    def col_copy(seq, j):
+        peer, device = col_peer(j)
+        return remote(
+            work.at[seq, piece(peer)], got.at[seq, col_me], col_send.at[seq, j], col_recv.at[seq, j], device
+        )
+
+    def grp_copy(seq, j):
+        peer, device = grp_peer(j)
+        return remote(
+            ready.at[seq, peer], land.at[seq, grp_me], grp_send.at[seq, j], grp_recv.at[seq, j], device
+        )
+
+    def red_copy(j):
+        return remote(mine, theirs.at[grp_me], red_send.at[j], red_recv.at[j], grp_peer(j)[1])
+
+    def late_copy(step):
+        return remote(
+            late.at[step], late_in.at[step], late_send.at[step], late_recv.at[step], (far_id, core_id)[step]
+        )
+
+    def pair(low, high):
+        return low + high, low - high
+
+    def four(values):
+        a, b = pair(values[0], values[2])
+        c, d = pair(values[1], values[3])
+        first, second = pair(a, c)
+        third, fourth = pair(b, d)
+        return first, second, third, fourth
+
+    def mix_local(seq):
+        @pl.loop(0, 4)
+        def _(q):
+            rows = pl.ds(pl.multiple_of(q * 8, 8), 8)
+            for half in range(2):
+                columns = slice(half * 256, half * 256 + 256)
+                upper = slice(512 + half * 256, 768 + half * 256)
+                left = four([sums[seq, a, rows, columns] for a in range(4)])
+                right = four([sums[seq, a, rows, upper] for a in range(4)])
+                for a in range(4):
+                    low, high = pair(left[a], right[a])
+                    work[seq, pl.ds(pl.multiple_of(q * 32 + a * 8, 8), 8), columns] = low
+                    work[seq, pl.ds(pl.multiple_of(128 + q * 32 + a * 8, 8), 8), columns] = high
+
+        values = work[seq]
+        coarse = values.astype(jnp.bfloat16)
+        fine = (values - coarse.astype(jnp.float32)).astype(jnp.bfloat16)
+        mixed = jnp.dot(coarse, walsh[...], preferred_element_type=jnp.float32)
+        mixed += jnp.dot(fine, walsh[...], preferred_element_type=jnp.float32)
+        work[seq] = mixed * (1.0 / D)
+
+    def mix_cols(seq):
+        @pl.loop(0, 4)
+        def _(o):
+            for part in range(2):
+                columns = slice(part * 256, part * 256 + 256)
+                rows = pl.ds(pl.multiple_of(o * 8, 8), 8)
+                left = four([got[seq, src, rows, columns] for src in range(4)])
+                right = four([got[seq, 4 + src, rows, columns] for src in range(4)])
+                for c in range(4):
+                    low, high = pair(left[c], right[c])
+                    ready[seq, o * 4 + c, :, columns] = low
+                    ready[seq, 16 + o * 4 + c, :, columns] = high
+
+    for seq in range(SEQS):
+        mix_local(seq)
+        if seq == 0:
+            pl.semaphore_wait(barrier, 39)
+
+        @pl.loop(1, 8)
+        def _(j):
+            col_copy(seq, j).start()
+
+        got[seq, col_me] = work[seq, piece(col_me)]
+
+    for seq in range(SEQS):
+
+        @pl.loop(1, 8)
+        def _(j):
+            col_copy(seq, j).wait_recv()
+
+        mix_cols(seq)
+
+        @pl.loop(1, 32)
+        def _(j):
+            grp_copy(seq, j).start()
+
+        land[seq, grp_me] = ready[seq, grp_me]
+
+    mine[...] = jnp.zeros((8, 128), jnp.float32)
+    for seq in range(SEQS):
+
+        @pl.loop(1, 32)
+        def _(j):
+            grp_copy(seq, j).wait_recv()
+
+        def add(i, carry):
+            rows = pl.ds(pl.multiple_of(i * 8, 8), 8)
+            value = land[seq, i]
+            other = chosen[seq, rows]
+            out[seq, rows] = value
+            terms = (value * other, value * value, other * other)
+            return tuple(total + term for total, term in zip(carry, terms))
+
+        start = tuple(jnp.zeros((8, 512), jnp.float32) for _ in range(3))
+        for kind, total in enumerate(lax.fori_loop(0, 32, add, start)):
+            total = total[:, 0:128] + total[:, 128:256] + total[:, 256:384] + total[:, 384:512]
+            mine[2 * kind + seq : 2 * kind + seq + 1, :] = jnp.sum(total, axis=0, keepdims=True)
+
+    @pl.loop(1, 32)
+    def _(j):
+        red_copy(j).start()
+
+    theirs[grp_me] = mine[...]
+
+    @pl.loop(1, 32)
+    def _(j):
+        red_copy(j).wait_recv()
+
+    late[0] = lax.fori_loop(0, 32, lambda i, total: total + theirs[i], jnp.zeros((8, 128), jnp.float32))
+    for step in range(2):
+        late_copy(step).start()
+        late_copy(step).wait_recv()
+        both = late[step] + late_in[step]
+        if step == 0:
+            late[1] = both
+    totals[...] = jnp.broadcast_to(jnp.sum(both, axis=1, keepdims=True), (8, 128))
+
+    for seq in range(SEQS):
+
+        @pl.loop(1, 8)
+        def _(j):
+            col_copy(seq, j).wait_send()
+
+        @pl.loop(1, 32)
+        def _(j):
+            grp_copy(seq, j).wait_send()
+
+    @pl.loop(1, 32)
+    def _(j):
+        red_copy(j).wait_send()
+
+    for step in range(2):
+        late_copy(step).wait_send()
+
+
+def mixed_prints(sums, chosen, walsh):
+    dma = pltpu.SemaphoreType.DMA
+    vmem = pl.BlockSpec(memory_space=pltpu.VMEM)
+    return pl.pallas_call(
+        mix_kernel,
+        out_shape=(
+            jax.ShapeDtypeStruct((SEQS, 256, 512), jnp.float32),
+            jax.ShapeDtypeStruct((8, 128), jnp.float32),
+        ),
+        in_specs=[vmem, vmem, vmem],
+        out_specs=(vmem, vmem),
+        scratch_shapes=[
+            pltpu.VMEM((SEQS, 256, 512), jnp.float32),
+            pltpu.VMEM((SEQS, 8, 32, 512), jnp.float32),
+            pltpu.VMEM((SEQS, 32, 8, 512), jnp.float32),
+            pltpu.VMEM((SEQS, 32, 8, 512), jnp.float32),
+            pltpu.VMEM((8, 128), jnp.float32),
+            pltpu.VMEM((32, 8, 128), jnp.float32),
+            pltpu.VMEM((2, 8, 128), jnp.float32),
+            pltpu.VMEM((2, 8, 128), jnp.float32),
+            dma((SEQS, 8)),
+            dma((SEQS, 8)),
+            dma((SEQS, 32)),
+            dma((SEQS, 32)),
+            dma((32,)),
+            dma((32,)),
+            dma((2,)),
+            dma((2,)),
+        ],
+        compiler_params=pltpu.CompilerParams(
+            collective_id=1, has_side_effects=True, vmem_limit_bytes=32 * 1024 * 1024
+        ),
+    )(sums, chosen, walsh)
 
 
 def body(activations, out_grads, token_mask, row_signs, col_signs, bank, bank_index):
     squared = float(D) * float(D)
-    y_hi = lax.axis_index("col_0")
-    all_signs = lax.all_gather(row_signs, TOK, axis=0, tiled=True)
-    mine = lax.dynamic_slice_in_dim(all_signs, y_hi * 2048, 2048, 0)
-    signs = (2 * mine - 1).astype(jnp.float32).reshape(8, 1, 256)
-    tables = (hadamard(256)[None] * signs).astype(jnp.bfloat16)
     col_pm = (2 * col_signs - 1).astype(jnp.bfloat16)
     grads = out_grads * token_mask[:, :, None].astype(jnp.bfloat16) * col_pm[None, None, :]
-
-    sums = gathered_products(activations, grads, tables)
-
-    sums = jnp.einsum("am,sapc->smpc", hadamard(4), sums, precision=HIGH)
-    sums = sums.reshape(SEQS, 4, 32, 2, 512)
-    sums = jnp.einsum("yh,smpyc->smphc", hadamard(2), sums, precision=HIGH)
-    sums = jnp.dot(sums, hadamard(512), precision=HIGH) * (1.0 / D)
-    pieces = sums.reshape(SEQS, 4, 4, 8, 2, 512).transpose(4, 2, 0, 1, 3, 5).reshape(8, SEQS, 4, 8, 512)
-    pieces = lax.all_to_all(pieces, COL, split_axis=0, concat_axis=0, tiled=True)
-    pieces = jnp.einsum("ab,bsmpc->asmpc", hadamard(8), pieces, precision=HIGH)
-    pieces = pieces.reshape(2, 4, SEQS, 4, 8, 512).transpose(0, 3, 1, 2, 4, 5).reshape(32, SEQS, 8, 512)
-    pieces = lax.all_to_all(pieces, ("tok_0", "tok_1", "col_1"), split_axis=0, concat_axis=0, tiled=True)
-    prints = pieces.transpose(1, 0, 2, 3).reshape(SEQS, 256, 512)
-
+    sums = gathered_products(activations, grads, row_signs.reshape(1, 256), hadamard(256))
     chosen = jnp.stack(
         [lax.dynamic_index_in_dim(bank, bank_index[seq], 0, keepdims=False) for seq in range(SEQS)]
     )
-    totals = jnp.concatenate(
-        [
-            jnp.sum(prints * chosen, axis=(1, 2)),
-            jnp.sum(prints * prints, axis=(1, 2)),
-            jnp.sum(chosen * chosen, axis=(1, 2)),
-        ]
-    )
-    totals = lax.psum(totals, EVERY)
-    cross, own, refsq = totals[0:2], totals[2:4], totals[4:6]
+    prints, totals = mixed_prints(sums, chosen, hadamard(512).astype(jnp.bfloat16))
+    cross, own, refsq = totals[0:2, 0], totals[2:4, 0], totals[4:6, 0]
     scores = D * (cross / squared) / jnp.sqrt((own / squared + 1e-06) * (refsq / squared + 1e-06))
     return prints, scores
 

time: 306 us -> 224 us (0.73)
  blocking collectives: 104 us -> 0 us
  Pallas kernels: 158 us -> 207 us
  matrix products: 12.6 us -> 0 us
  waiting for transfers between devices: 6.78 us -> 0 us
  starting transfers between devices: 5.44 us -> 0 us
    psum x1 -> x0, blocking collectives: 66.2 us -> none  [body(): totals = lax.psum(totals, EVERY)]
    pallas_call x0 -> x1, Pallas kernels: none -> 48.9 us  [mixed_prints(): pl.pallas_call(mix_kernel, out_shape=(jax.ShapeDtypeStruct((SEQS, 256, 51...]
    all_gather x1 -> x0, blocking collectives: 21.3 us -> none  [body(): all_signs = lax.all_gather(row_signs, TOK, axis=0, tiled=True)]
    all_to_all x1 -> x0, blocking collectives: 16.9 us -> none  [body(): lax.all_to_all(pieces, COL, split_axis=0, concat_axis=0, tiled=True)]
    dot_general x4 -> x0, matrix products: 12.6 us -> none  [the longest x1 4.01 us: body(): sums = jnp.einsum('yh,smpyc->smphc', hadamard(2), sums, precision=HIGH)]
    all_to_all x1 -> x0, waiting for transfers between devices: 6.78 us -> none  [body(): lax.all_to_all(pieces, ('tok_0', 'tok_1', 'col_1'), split_axis=0, concat_...]
    all_to_all x1 -> x0, starting transfers between devices: 5.44 us -> none  [body(): lax.all_to_all(pieces, ('tok_0', 'tok_1', 'col_1'), split_axis=0, concat_...]
    reshape x4 -> x0, local copies, waits for them, and re-layouts: 4.01 us -> none  [the longest x2 1.89 us: body(): pieces.reshape(2, 4, SEQS, 4, 8, 512).transpose(0, 3, 1, 2, 4, 5)]
  transfers between devices with their start and end apart: 1 -> 0, of which waited for: 1 -> 0; matrix products, arithmetic and copies ran while one was open for 1% -> 0% of each run, Pallas kernels for 0% -> 0%
where the time goes in v2:
time: 224 us; the launch traced here: 223 us
  Pallas kernels  207 us (92%)
  other arithmetic  7.92 us (4%)
  between operations  4.56 us (2%)
  local copies, waits for them, and re-layouts  3.59 us (2%)
    pallas_call x1, Pallas kernels, gathered_products(): pl.pallas_call(gather_kernel, out_shape=jax.ShapeDtypeStruct((SEQS, BLOCK...  158 us
    pallas_call x1, Pallas kernels, mixed_prints(): pl.pallas_call(mix_kernel, out_shape=(jax.ShapeDtypeStruct((SEQS, 256, 51...  48.9 us

profile of v2, /device:TPU:1, one launch (start us, length us, event | category | flops | bytes accessed | tf_op | source)
XLA Modules:
  0.0 223.3 jit_solution(12934844968850323615)
XLA Ops:
  0.6 0.7 add_convert_fusion
  1.3 0.7 convert_element_type.16
  2.0 3.3 %multiply_multiply_fusion.grads = bf16[2,1536,512]{2,1,0:T(8,128)(2,1)} fusion(bf16[2,1536,512]{2,1,0:T(8,128)(2,1)} %param.8, bf16[512]{0:T(512)(128)(2,1)S(1)} %add_convert_fusion, bf16[2,1536]{1,0:T(2,128)(2,1)S(1)} %convert_element_type.16), kind=kLoop, calls=%fused_computation | loop fusion | flops 3145728 | bytes 6298624 | tf_op jit(solution)/shard_map/mul | solution.py:649
  5.4 1.0 fusion.8.walsh
  6.4 158.4 %shard_map.86.sums = f32[2,4,32,1024]{3,2,1,0:T(8,128)} custom-call(bf16[2,1536,512]{2,1,0:T(8,128)(2,1)} %acts.1, bf16[2,1536,512]{2,1,0:T(8,128)(2,1)} %multiply_multiply_fusion.grads, s32[1,256]{1,0:T(1,128)} %bitcast.3, f32[256,256]{1,0:T(8,128)} %fusion.8.walsh), custom_call_target="tpu_custom_call" | custom-call | tf_op jit(solution)/shard_map/pallas_call | solution.py:355
  164.8 0.0 copy-start
  164.8 1.3 fusion.9
  170.0 1.3 constant_dynamic-slice_fusion.1
  171.3 0.1 pad_maximum_fusion.chosen
  171.4 1.4 fusion.4.walsh
  172.8 0.0 copy-done
  172.8 48.9 %shard_map.87 = (f32[2,256,512]{2,1,0:T(8,128)S(1)}, f32[8,128]{1,0:T(8,128)S(1)}) custom-call(f32[2,4,32,1024]{3,2,1,0:T(8,128)S(1)} %copy-done, f32[2,256,512]{2,1,0:T(8,128)S(1)} %pad_maximum_fusion.chosen, bf16[512,512]{1,0:T(8,128)(2,1)S(1)} %fusion.4.walsh), custom_call_target="tpu_custom_call" | custom-call | tf_op jit(solution)/shard_map/pallas_call | solution.py:614
  221.7 0.6 multiply_reduce_fusion
  222.3 1.0 copy.10
Async XLA Ops:
  164.8 8.0 %copy-start = (f32[2,4,32,1024]{3,2,1,0:T(8,128)S(1)}, f32[2,4,32,1024]{3,2,1,0:T(8,128)}, u32[]{:S(2)}) copy-start(f32[2,4,32,1024]{3,2,1,0:T(8,128)} %shard_map.86.sums) | copy-start | bytes 3145732

commit v3 on v2

--- a/solution.py
+++ b/solution.py
@@ -20,30 +20,117 @@
 HALF = TOKENS // 2
 FEATS = 512
 BLOCKS = 4
-UNITS = SEQS * BLOCKS
-
-
-def hadamard(order):
-    positions = jnp.arange(order, dtype=jnp.int32)
-    common_bits = jnp.bitwise_and(positions[:, None], positions[None, :])
-    parity = jnp.zeros((order, order), jnp.int32)
-    for bit_number in range(max(order.bit_length() - 1, 0)):
-        parity = parity + jnp.bitwise_and(jnp.right_shift(common_bits, bit_number), 1)
-    return (1 - 2 * (parity % 2)).astype(jnp.float32)
+UNITS = SEQS * BLOCKS * 2
+
+ORDER = (
+    ('run', 0, 0, 0),
+    ('run', 1, 0, 0),
+    ('core', 0, 0, 0),
+    ('core', 1, 0, 0),
+    ('half', 0, 0, 0),
+    ('half', 1, 0, 0),
+    ('spass', 0),
+    ('rpass', 0),
+    ('full', 0, 0, 0),
+    ('full', 1, 0, 0),
+    ('run', 0, 3, 0),
+    ('run', 0, 0, 1),
+    ('core', 0, 3, 0),
+    ('run', 0, 3, 1),
+    ('core', 0, 0, 1),
+    ('run', 0, 1, 0),
+    ('half', 0, 3, 0),
+    ('core', 0, 3, 1),
+    ('run', 0, 1, 1),
+    ('half', 0, 0, 1),
+    ('core', 0, 1, 0),
+    ('core', 0, 1, 1),
+    ('full', 0, 3, 0),
+    ('half', 0, 3, 1),
+    ('run', 0, 2, 0),
+    ('spass', 1),
+    ('full', 0, 0, 1),
+    ('run', 0, 2, 1),
+    ('half', 0, 1, 0),
+    ('core', 0, 2, 0),
+    ('half', 0, 1, 1),
+    ('end', 0, 0, 0),
+    ('end', 1, 0, 0),
+    ('end', 0, 3, 0),
+    ('core', 0, 2, 1),
+    ('full', 0, 3, 1),
+    ('full', 0, 1, 0),
+    ('half', 0, 2, 0),
+    ('full', 0, 1, 1),
+    ('half', 0, 2, 1),
+    ('rpass', 1),
+    ('full', 0, 2, 0),
+    ('full', 0, 2, 1),
+    ('run', 1, 0, 1),
+    ('end', 0, 0, 1),
+    ('end', 0, 3, 1),
+    ('core', 1, 0, 1),
+    ('end', 0, 1, 0),
+    ('end', 0, 1, 1),
+    ('end', 0, 2, 0),
+    ('half', 1, 0, 1),
+    ('end', 0, 2, 1),
+    ('run', 1, 3, 0),
+    ('full', 1, 0, 1),
+    ('run', 1, 3, 1),
+    ('core', 1, 3, 0),
+    ('run', 1, 1, 0),
+    ('core', 1, 3, 1),
+    ('run', 1, 1, 1),
+    ('half', 1, 3, 0),
+    ('core', 1, 1, 0),
+    ('end', 1, 0, 1),
+    ('half', 1, 3, 1),
+    ('core', 1, 1, 1),
+    ('full', 1, 3, 0),
+    ('half', 1, 1, 0),
+    ('run', 1, 2, 0),
+    ('run', 1, 2, 1),
+    ('full', 1, 3, 1),
+    ('half', 1, 1, 1),
+    ('core', 1, 2, 0),
+    ('end', 1, 3, 0),
+    ('core', 1, 2, 1),
+    ('full', 1, 1, 0),
+    ('end', 1, 3, 1),
+    ('full', 1, 1, 1),
+    ('end', 1, 1, 0),
+    ('half', 1, 2, 0),
+    ('half', 1, 2, 1),
+    ('end', 1, 1, 1),
+    ('full', 1, 2, 0),
+    ('full', 1, 2, 1),
+    ('end', 1, 2, 0),
+    ('end', 1, 2, 1),
+)
+
+
+def hadamard_rows(first, rows, order):
+    down = lax.broadcasted_iota(jnp.int32, (rows, order), 0) + first
+    common_bits = jnp.bitwise_and(down, lax.broadcasted_iota(jnp.int32, (rows, order), 1))
+    for shift in (8, 4, 2, 1):
+        common_bits = jnp.bitwise_xor(common_bits, jnp.right_shift(common_bits, shift))
+    return (1 - 2 * jnp.bitwise_and(common_bits, 1)).astype(jnp.float32)
 
 
 def gather_kernel(
     acts,
     grads,
     row_bits,
-    walsh,
+    col_bits,
+    mask,
     out,
     bits,
+    walsh,
     tables,
     a_buf,
     m_buf,
     relay,
-    turned,
     part,
     core_in,
     x_half,
@@ -84,12 +171,10 @@
     core_id = (x, y_lo, 1 - core, y_hi, z)
     pair_id = (x, 1 - y_lo, core, y_hi, z)
 
-    loads = []
-    for seq in range(SEQS):
-        loads.append(pltpu.make_async_copy(acts.at[seq], a_buf.at[seq, 0], load_sem.at[2 * seq]))
-        loads.append(pltpu.make_async_copy(grads.at[seq], m_buf.at[seq, 0], load_sem.at[2 * seq + 1]))
-    loads.append(pltpu.make_async_copy(row_bits, bits.at[y_lo, x, core], bit_load))
-    for copy in loads:
+    bit_own = pltpu.make_async_copy(row_bits, bits.at[core, x, y_lo], bit_load)
+    m_own = [pltpu.make_async_copy(grads.at[seq], m_buf.at[seq, 0], load_sem.at[seq]) for seq in range(SEQS)]
+    a_own = [pltpu.make_async_copy(acts.at[seq], a_buf.at[seq, 0], load_sem.at[2 + seq]) for seq in range(SEQS)]
+    for copy in (bit_own, *m_own, *a_own):
         copy.start()
 
     barrier = pltpu.get_barrier_semaphore()
@@ -114,7 +199,7 @@
 
     def swap_copy(seq, way, hop):
         index = (seq * 2 + way) * 2 + hop
-        src = relay.at[seq, way] if hop else grads.at[seq, rows_of(way)]
+        src = relay.at[seq, way] if hop else m_buf.at[seq, 0, rows_of(way)]
         dst = m_buf.at[seq, 1, rows_of(way)] if hop else relay.at[seq, way]
         return remote(src, dst, m_send.at[index], m_recv.at[index], y_ids[way])
 
@@ -158,52 +243,52 @@
         return remote(ref, ref, bit_send.at[index], bit_recv.at[index], device)
 
     def share_bits():
-        loads.pop().wait()
-        start(bit_copy(0, bits.at[y_lo, x, core], core_id))
-        bit_copy(0, bits.at[y_lo, x, core], core_id).wait_recv()
-        for way in range(2):
-            start(bit_copy(1 + way, bits.at[y_lo, x], x_ids[way]))
-        for way in range(2):
-            bit_copy(1 + way, bits.at[y_lo, x], x_ids[way]).wait_recv()
-        start(bit_copy(3, bits.at[y_lo, x_prev], x_ids[0]))
-        bit_copy(3, bits.at[y_lo, x_prev], x_ids[0]).wait_recv()
-        start(bit_copy(4, bits.at[y_lo], pair_id))
+        for way in range(2):
+            start(bit_copy(1 + way, bits.at[core, x], x_ids[way]))
+        for way in range(2):
+            bit_copy(1 + way, bits.at[core, x], x_ids[way]).wait_recv()
+        start(bit_copy(3, bits.at[core, x_prev], x_ids[0]))
+        bit_copy(3, bits.at[core, x_prev], x_ids[0]).wait_recv()
+        start(bit_copy(4, bits.at[core], core_id))
 
     def sign_tables():
-        bit_copy(4, bits.at[y_lo], pair_id).wait_recv()
+        bit_copy(4, bits.at[core], core_id).wait_recv()
 
         @pl.loop(0, 8)
         def _(i):
-            row = bits[lax.rem(lax.div(i, 2), 2), 2 * y_hi + lax.div(i, 4), lax.rem(i, 2)]
+            row = bits[lax.rem(i, 2), 2 * y_hi + lax.div(i, 4), lax.rem(lax.div(i, 2), 2)]
             signs = (2 * row - 1).astype(jnp.float32)
             tables[i] = (walsh[...] * signs).astype(jnp.bfloat16)
 
+    def column_signs(seq):
+        signs = (2 * col_bits[...] - 1).astype(jnp.float32).astype(jnp.bfloat16)
+
+        @pl.loop(0, TOKENS // 32)
+        def _(i):
+            rows = pl.ds(pl.multiple_of(i * 32, 32), 32)
+            m_buf[seq, 0, rows] = m_buf[seq, 0, rows] * signs
+
     core_sign = (1 - 2 * core).astype(jnp.float32)
 
-    def compute(unit, seq, slot):
+    def compute(unit, seq, slot, m):
         block = lax.rem(z + slot, 4)
+        counted = mask[seq].astype(jnp.float32).astype(jnp.bfloat16)
 
         @pl.loop(0, 2)
         def _(b):
             columns = pl.ds(pl.multiple_of(b * 256, 256), 256)
-            turned[b] = a_buf[seq, slot, :, columns].T
-
-        @pl.loop(0, 4)
-        def _(i):
-            b = lax.div(i, 2)
-            m = lax.rem(i, 2)
-            tile = jnp.dot(turned[b], m_buf[seq, m], preferred_element_type=jnp.float32)
+            rows_first = a_buf[seq, slot, :, columns].T * counted
+            tile = jnp.dot(rows_first, m_buf[seq, m], preferred_element_type=jnp.float32)
             coarse = tile.astype(jnp.bfloat16)
             fine = (tile - coarse.astype(jnp.float32)).astype(jnp.bfloat16)
             table = tables[2 * block + b]
             mixed = jnp.dot(table, coarse, preferred_element_type=jnp.float32)
             mixed += jnp.dot(table, fine, preferred_element_type=jnp.float32)
-            columns = pl.ds(pl.multiple_of(lax.rem(m + y_hi, 2) * 512, 512), 512)
-            part[unit, b, :, columns] = mixed
-
-        @pl.loop(0, 32)
+            part[unit, b] = mixed
+
+        @pl.loop(0, 16)
         def _(i):
-            rows = pl.ds(pl.multiple_of(i * 8, 8), 8)
+            rows = pl.ds(pl.multiple_of(i * 16, 16), 16)
             low = part[unit, 0, rows]
             high = part[unit, 1, rows] * core_sign
             part[unit, 0, rows] = low + high
@@ -272,85 +357,72 @@
 
         start(y_copy(unit))
 
-    def finish(unit, seq, slot):
+    def finish(unit, seq, slot, m):
         block = lax.rem(z + slot, 4)
+        columns = pl.ds(pl.multiple_of(lax.rem(m + y_hi, 2) * FEATS, FEATS), FEATS)
         y_copy(unit).wait_recv()
 
         @pl.loop(0, 4)
         def _(i):
             here = pl.ds(pl.multiple_of(i * 8, 8), 8)
             there = pl.ds(pl.multiple_of(x * 64 + y_lo * 32 + i * 8, 8), 8)
-            out[seq, block, here] = part[unit, 0, there] + y_in[unit, here]
-
-    order = [(seq, slot) for seq in range(SEQS) for slot in (0, 3, 1, 2)]
-    run = [functools.partial(compute, unit, *order[unit]) for unit in range(UNITS)]
-    end = [functools.partial(finish, unit, *order[unit]) for unit in range(UNITS)]
+            out[seq, block, here, columns] = part[unit, 0, there] + y_in[unit, here]
 
     ring_own(0)
+    walsh[...] = hadamard_rows(0, 256, 256)
+    bit_own.wait()
+    start(bit_copy(0, bits.at[core, x, y_lo], pair_id))
+    m_own[0].wait()
+    column_signs(0)
     swap_own(0)
+    bit_copy(0, bits.at[core, x, y_lo], pair_id).wait_recv()
     share_bits()
-    swap_pass(0)
-    swap_own(1)
-    ring_pass(0)
-    ring_own(1)
-    for copy in loads:
+    m_own[1].wait()
+    column_signs(1)
+    for copy in a_own:
         copy.wait()
     sign_tables()
-    swap_end(0)
-    run[0]()
-    ring_near(0, 0)
-    run[1]()
-    sum_core(0)
-    ring_near(0, 1)
-    run[2]()
-    sum_core(1)
-    sum_half(0)
-    sum_core(2)
-    sum_half(1)
-    swap_pass(1)
-    sum_full(0)
-    sum_half(2)
-    ring_far(0)
-    run[3]()
-    sum_core(3)
-    sum_full(1)
-    end[0]()
-    sum_half(3)
-    sum_full(2)
-    end[1]()
-    ring_pass(1)
-    swap_end(1)
-    run[4]()
-    sum_core(4)
-    sum_full(3)
-    end[2]()
-    sum_half(4)
-    end[3]()
-    sum_full(4)
-    ring_near(1, 0)
-    run[5]()
-    ring_near(1, 1)
-    run[6]()
-    sum_core(5)
-    sum_core(6)
-    sum_half(5)
-    sum_half(6)
-    end[4]()
-    sum_full(5)
-    sum_full(6)
-    ring_far(1)
-    run[7]()
-    sum_core(7)
-    end[5]()
-    end[6]()
-    sum_half(7)
-    sum_full(7)
-    end[7]()
+
+    here = {("a", 0, 0), ("a", 1, 0), ("m", 0, 0), ("m", 1, 0)}
+
+    def once(key, wait):
+        if key not in here:
+            here.add(key)
+            wait()
+
+    for step, *rest in ORDER:
+        if step == "spass":
+            swap_pass(rest[0])
+            if rest[0] == 0:
+                swap_own(1)
+            continue
+        if step == "rpass":
+            ring_pass(rest[0])
+            if rest[0] == 0:
+                ring_own(1)
+            continue
+        seq, slot, m = rest
+        unit = (seq * BLOCKS + slot) * 2 + m
+        if step == "run":
+            if slot == 2:
+                once(("a", seq, 2), lambda seq=seq: ring_far(seq))
+            else:
+                once(("a", seq, slot), lambda seq=seq, slot=slot: ring_near(seq, 0 if slot == 3 else 1))
+            once(("m", seq, m), lambda seq=seq: swap_end(seq))
+            compute(unit, seq, slot, m)
+        elif step == "core":
+            sum_core(unit)
+        elif step == "half":
+            sum_half(unit)
+        elif step == "full":
+            sum_full(unit)
+        else:
+            finish(unit, seq, slot, m)
     for copy in sent:
         copy.wait_send()
 
 
-def gathered_products(acts, grads, row_bits, walsh):
+def gathered_products(acts, grads, row_bits, col_bits, mask):
     dma = pltpu.SemaphoreType.DMA
     return pl.pallas_call(
         gather_kernel,
@@ -360,20 +432,21 @@
             pl.BlockSpec(memory_space=pl.ANY),
             pl.BlockSpec(memory_space=pl.ANY),
             pl.BlockSpec(memory_space=pltpu.VMEM),
+            pl.BlockSpec(memory_space=pltpu.VMEM),
         ],
         out_specs=pl.BlockSpec(memory_space=pltpu.VMEM),
         scratch_shapes=[
             pltpu.VMEM((2, 4, 2, 1, 256), jnp.int32),
+            pltpu.VMEM((256, 256), jnp.float32),
             pltpu.VMEM((8, 256, 256), jnp.bfloat16),
             pltpu.VMEM((SEQS, BLOCKS, TOKENS, FEATS), jnp.bfloat16),
             pltpu.VMEM((SEQS, 2, TOKENS, FEATS), jnp.bfloat16),
             pltpu.VMEM((SEQS, 2, HALF, FEATS), jnp.bfloat16),
-            pltpu.VMEM((2, 256, TOKENS), jnp.bfloat16),
-            pltpu.VMEM((UNITS, 2, 256, 2 * FEATS), jnp.float32),
-            pltpu.VMEM((UNITS, 256, 2 * FEATS), jnp.float32),
-            pltpu.VMEM((UNITS, 2, 32, 2 * FEATS), jnp.float32),
-            pltpu.VMEM((UNITS, 2, 64, 2 * FEATS), jnp.float32),
-            pltpu.VMEM((UNITS, 32, 2 * FEATS), jnp.float32),
+            pltpu.VMEM((UNITS, 2, 256, FEATS), jnp.float32),
+            pltpu.VMEM((UNITS, 256, FEATS), jnp.float32),
+            pltpu.VMEM((UNITS, 2, 32, FEATS), jnp.float32),
+            pltpu.VMEM((UNITS, 2, 64, FEATS), jnp.float32),
+            pltpu.VMEM((UNITS, 32, FEATS), jnp.float32),
             dma((4,)),
             dma((12,)),
             dma((12,)),
@@ -394,15 +467,16 @@
         compiler_params=pltpu.CompilerParams(
             collective_id=0, has_side_effects=True, vmem_limit_bytes=67043328
         ),
-    )(acts, grads, row_bits, walsh)
+    )(acts, grads, row_bits, col_bits, mask)
 
 
 def mix_kernel(
     sums,
-    chosen,
-    walsh,
+    chosen_0,
+    chosen_1,
     out,
     totals,
+    walsh,
     work,
     got,
     ready,
@@ -454,6 +528,11 @@
 
     pl.semaphore_signal(barrier, inc=1, device_id=core_id, device_id_type=MESH)
 
+    @pl.loop(0, 8)
+    def _(i):
+        rows = pl.ds(pl.multiple_of(i * 64, 64), 64)
+        walsh[rows] = hadamard_rows(i * 64, 64, 512).astype(jnp.bfloat16)
+
     def remote(src, dst, send, recv, device):
         return pltpu.make_async_remote_copy(
             src_ref=src, dst_ref=dst, send_sem=send, recv_sem=recv, device_id=device, device_id_type=MESH
@@ -561,7 +640,7 @@
         def add(i, carry):
             rows = pl.ds(pl.multiple_of(i * 8, 8), 8)
             value = land[seq, i]
-            other = chosen[seq, rows]
+            other = (chosen_0, chosen_1)[seq][rows]
             out[seq, rows] = value
             terms = (value * other, value * value, other * other)
             return tuple(total + term for total, term in zip(carry, terms))
@@ -608,7 +687,7 @@
         late_copy(step).wait_send()
 
 
-def mixed_prints(sums, chosen, walsh):
+def mixed_prints(sums, chosen_0, chosen_1):
     dma = pltpu.SemaphoreType.DMA
     vmem = pl.BlockSpec(memory_space=pltpu.VMEM)
     return pl.pallas_call(
@@ -620,6 +699,7 @@
         in_specs=[vmem, vmem, vmem],
         out_specs=(vmem, vmem),
         scratch_shapes=[
+            pltpu.VMEM((512, 512), jnp.bfloat16),
             pltpu.VMEM((SEQS, 256, 512), jnp.float32),
             pltpu.VMEM((SEQS, 8, 32, 512), jnp.float32),
             pltpu.VMEM((SEQS, 32, 8, 512), jnp.float32),
@@ -640,18 +720,23 @@
         compiler_params=pltpu.CompilerParams(
             collective_id=1, has_side_effects=True, vmem_limit_bytes=32 * 1024 * 1024
         ),
-    )(sums, chosen, walsh)
+    )(sums, chosen_0, chosen_1)
 
 
 def body(activations, out_grads, token_mask, row_signs, col_signs, bank, bank_index):
     squared = float(D) * float(D)
-    col_pm = (2 * col_signs - 1).astype(jnp.bfloat16)
-    grads = out_grads * token_mask[:, :, None].astype(jnp.bfloat16) * col_pm[None, None, :]
-    sums = gathered_products(activations, grads, row_signs.reshape(1, 256), hadamard(256))
-    chosen = jnp.stack(
-        [lax.dynamic_index_in_dim(bank, bank_index[seq], 0, keepdims=False) for seq in range(SEQS)]
+    sums = gathered_products(
+        activations,
+        out_grads,
+        row_signs.reshape(1, 256),
+        col_signs.reshape(1, FEATS),
+        token_mask.reshape(SEQS, 1, TOKENS),
     )
-    prints, totals = mixed_prints(sums, chosen, hadamard(512).astype(jnp.bfloat16))
+    chosen = [
+        lax.dynamic_index_in_dim(bank, bank_index[seq], 0, keepdims=False, allow_negative_indices=False)
+        for seq in range(SEQS)
+    ]
+    prints, totals = mixed_prints(sums, *chosen)
     cross, own, refsq = totals[0:2, 0], totals[2:4, 0], totals[4:6, 0]
     scores = D * (cross / squared) / jnp.sqrt((own / squared + 1e-06) * (refsq / squared + 1e-06))
     return prints, scores

time: 224 us -> 192 us (0.86)
  Pallas kernels: 207 us -> 183 us
  other arithmetic: 7.92 us -> 0.64 us
  between operations: 4.56 us -> 0.66 us
  local copies, waits for them, and re-layouts: 3.59 us -> 7.37 us
    pallas_call x1, Pallas kernels: 158 us -> 135 us  [gathered_products(): pl.pallas_call(gather_kernel, out_shape=jax.ShapeDtypeStruct((SEQS, BLOCK...]
    convert_element_type x4 -> x0, other arithmetic: 3.86 us -> none  [the longest x1 1.43 us: body(): hadamard(512).astype(jnp.bfloat16)]
    mul x1 -> x0, other arithmetic: 3.35 us -> none  [body(): out_grads * token_mask[:, :, None].astype(jnp.bfloat16)]
    squeeze x0 -> x1, local copies, waits for them, and re-layouts: none -> 2.55 us  [body(): lax.dynamic_index_in_dim(bank, bank_index[seq], 0, keepdims=False, allow_...]
where the time goes in v3:
time: 192 us
  Pallas kernels  183 us (95%)
  local copies, waits for them, and re-layouts  7.37 us (4%)
    pallas_call x1, Pallas kernels, gathered_products(): pl.pallas_call(gather_kernel, out_shape=jax.ShapeDtypeStruct((SEQS, BLOCK...  135 us
    pallas_call x1, Pallas kernels, mixed_prints(): pl.pallas_call(mix_kernel, out_shape=(jax.ShapeDtypeStruct((SEQS, 256, 51...  48.2 us

profile of v3, /device:TPU:1, one launch (start us, length us, event | category | flops | bytes accessed | tf_op | source)
XLA Modules:
  0.0 191.7 jit_solution(7451640169124343677)
XLA Ops:
  0.6 1.3 fusion
  1.9 1.3 reshape.27.mask
  3.3 134.9 %shard_map.86.sums = f32[2,4,32,1024]{3,2,1,0:T(8,128)} custom-call(bf16[2,1536,512]{2,1,0:T(8,128)(2,1)} %acts.1, bf16[2,1536,512]{2,1,0:T(8,128)(2,1)} %grads.1, s32[1,256]{1,0:T(1,128)} %bitcast.9, s32[1,512]{1,0:T(1,128)} %bitcast.8, s32[2,1,1536]{2,1,0:T(1,128)} %reshape.27.mask), custom_call_target="tpu_custom_call" | custom-call | tf_op jit(solution)/shard_map/pallas_call | solution.py:427
  138.2 2.6 %dynamic-slice_bitcast_fusion = (f32[256,512]{1,0:T(8,128)S(1)}, f32[256,512]{1,0:T(8,128)S(1)}) fusion(f32[16,256,512]{2,1,0:T(8,128)} %param.12, s32[]{:T(128)} %bitcast.4, s32[]{:T(128)} %bitcast.2), kind=kLoop, calls=%fused_computation | loop fusion | bytes 2097160 | tf_op jit(solution)/shard_map/jit(dynamic_index_in_dim)/squeeze | solution.py:736
  140.7 0.0 copy-start
  140.7 1.2 copy-done
  142.0 48.2 %shard_map.87 = (f32[2,256,512]{2,1,0:T(8,128)S(1)}, f32[8,128]{1,0:T(8,128)S(1)}) custom-call(f32[2,4,32,1024]{3,2,1,0:T(8,128)S(1)} %copy-done, f32[256,512]{1,0:T(8,128)S(1)} %get-tuple-element.7.chosen_0, f32[256,512]{1,0:T(8,128)S(1)} %get-tuple-element.6.chosen_1), custom_call_target="tpu_custom_call" | custom-call | tf_op jit(solution)/shard_map/pallas_call | solution.py:693
  190.1 0.6 multiply_reduce_fusion
  190.8 1.0 copy.10
Async XLA Ops:
  140.7 1.2 copy-start

commit v4 on v3

v4 whole, which is shorter than its diff:
```python
import functools
import math

import jax
import jax.numpy as jnp
from jax import lax
from jax.experimental import pallas as pl
from jax.experimental.pallas import tpu as pltpu
from jax.sharding import Mesh
from jax.sharding import PartitionSpec as P

D = 4096
TOK = ("tok_0", "tok_1", "tok_2")
COL = ("col_0", "col_1")
EVERY = ("tok_0", "tok_1", "tok_2", "col_0", "col_1")
MESH = pl.DeviceIdType.MESH

SEQS = 2
TOKENS = 1536
HALF = TOKENS // 2
FEATS = 512
BLOCKS = 4
UNITS = SEQS * BLOCKS * 2

ORDER = (
    ('run', 0, 0, 0),
    ('run', 1, 0, 0),
    ('core', 0, 0, 0),
    ('core', 1, 0, 0),
    ('half', 0, 0, 0),
    ('half', 1, 0, 0),
    ('rpass', 0),
    ('full', 0, 0, 0),
    ('full', 1, 0, 0),
    ('end', 0, 0, 0),
    ('end', 1, 0, 0),
    ('run', 0, 3, 0),
    ('run', 0, 0, 1),
    ('core', 0, 3, 0),
    ('run', 0, 3, 1),
    ('core', 0, 0, 1),
    ('run', 0, 1, 0),
    ('core', 0, 3, 1),
    ('half', 0, 3, 0),
    ('run', 0, 1, 1),
    ('core', 0, 1, 0),
    ('half', 0, 0, 1),
    ('half', 0, 3, 1),
    ('core', 0, 1, 1),
    ('full', 0, 3, 0),
    ('run', 0, 2, 0),
    ('half', 0, 1, 0),
    ('run', 0, 2, 1),
    ('full', 0, 0, 1),
    ('core', 0, 2, 0),
    ('end', 0, 3, 0),
    ('full', 0, 3, 1),
    ('core', 0, 2, 1),
    ('half', 0, 1, 1),
    ('end', 0, 0, 1),
    ('end', 0, 3, 1),
    ('full', 0, 1, 0),
    ('half', 0, 2, 0),
    ('half', 0, 2, 1),
    ('end', 0, 1, 0),
    ('full', 0, 1, 1),
    ('rpass', 1),
    ('run', 1, 0, 1),
    ('full', 0, 2, 0),
    ('end', 0, 1, 1),
    ('full', 0, 2, 1),
    ('core', 1, 0, 1),
    ('end', 0, 2, 0),
    ('end', 0, 2, 1),
    ('half', 1, 0, 1),
    ('full', 1, 0, 1),
    ('run', 1, 3, 0),
    ('run', 1, 3, 1),
    ('core', 1, 3, 0),
    ('run', 1, 1, 0),
    ('core', 1, 3, 1),
    ('run', 1, 1, 1),
    ('core', 1, 1, 0),
    ('half', 1, 3, 0),
    ('end', 1, 0, 1),
    ('mix', 0),
    ('core', 1, 1, 1),
    ('half', 1, 3, 1),
    ('half', 1, 1, 0),
    ('full', 1, 3, 0),
    ('run', 1, 2, 0),
    ('half', 1, 1, 1),
    ('run', 1, 2, 1),
    ('full', 1, 3, 1),
    ('core', 1, 2, 0),
    ('end', 1, 3, 0),
    ('full', 1, 1, 0),
    ('core', 1, 2, 1),
    ('end', 1, 3, 1),
    ('full', 1, 1, 1),
    ('end', 1, 1, 0),
    ('half', 1, 2, 0),
    ('half', 1, 2, 1),
    ('end', 1, 1, 1),
    ('full', 1, 2, 0),
    ('full', 1, 2, 1),
    ('cols', 0),
    ('end', 1, 2, 0),
    ('end', 1, 2, 1),
    ('mix', 1),
    ('land', 0),
    ('cols', 1),
    ('land', 1),
)


def hadamard_rows(first, rows, order):
    down = lax.broadcasted_iota(jnp.int32, (rows, order), 0) + first
    common_bits = jnp.bitwise_and(down, lax.broadcasted_iota(jnp.int32, (rows, order), 1))
    for shift in (8, 4, 2, 1):
        common_bits = jnp.bitwise_xor(common_bits, jnp.right_shift(common_bits, shift))
    return (1 - 2 * jnp.bitwise_and(common_bits, 1)).astype(jnp.float32)


def gather_kernel(
    acts,
    grads,
    row_bits,
    col_bits,
    mask,
    chosen_0,
    chosen_1,
    out,
    totals,
    sums,
    bits,
    walsh,
    tables,
    a_buf,
    m_buf,
    part,
    core_in,
    x_half,
    x_full,
    y_in,
    load_sem,
    a_send,
    a_recv,
    m_send,
    m_recv,
    core_send,
    core_recv,
    xh_send,
    xh_recv,
    xf_send,
    xf_recv,
    y_send,
    y_recv,
    bit_load,
    bit_send,
    bit_recv,
    wide,
    work,
    got,
    ready,
    land,
    mine,
    theirs,
    late,
    col_send,
    col_recv,
    grp_send,
    grp_recv,
    red_send,
    red_recv,
    late_send,
    late_recv,
):
    x = lax.axis_index("tok_0")
    y_lo = lax.axis_index("tok_1")
    core = lax.axis_index("tok_2")
    y_hi = lax.axis_index("col_0")
    z = lax.axis_index("col_1")
    x_next, x_prev, x_far = lax.rem(x + 1, 4), lax.rem(x + 3, 4), lax.rem(x + 2, 4)
    z_ids = ((x, y_lo, core, y_hi, lax.rem(z + 1, 4)), (x, y_lo, core, y_hi, lax.rem(z + 3, 4)))
    x_ids = ((x_next, y_lo, core, y_hi, z), (x_prev, y_lo, core, y_hi, z))
    core_id = (x, y_lo, 1 - core, y_hi, z)
    pair_id = (x, 1 - y_lo, core, y_hi, z)
    far_id = (x, y_lo, core, 1 - y_hi, z)
    last_ids = (far_id, core_id, (x, y_lo, 1 - core, 1 - y_hi, z))
    col_me = y_hi * 4 + z
    grp_me = x * 8 + y_lo * 4 + z

    def col_peer(j):
        there_y = lax.rem(y_hi + lax.div(j, 4), 2)
        there_z = lax.rem(z + j, 4)
        return there_y * 4 + there_z, (x, y_lo, core, there_y, there_z)

    def grp_peer(j):
        there_x = lax.rem(x + lax.div(j, 8), 4)
        there_y = lax.rem(y_lo + lax.div(j, 4), 2)
        there_z = lax.rem(z + j, 4)
        return there_x * 8 + there_y * 4 + there_z, (there_x, there_y, core, y_hi, there_z)

    bit_own = pltpu.make_async_copy(row_bits, bits.at[core, x, y_lo], bit_load)
    m_own = [pltpu.make_async_copy(grads.at[seq], m_buf.at[seq, 0], load_sem.at[seq]) for seq in range(SEQS)]
    a_own = [pltpu.make_async_copy(acts.at[seq], a_buf.at[seq, 0], load_sem.at[2 + seq]) for seq in range(SEQS)]
    for copy in (bit_own, *m_own, *a_own):
        copy.start()

    barrier = pltpu.get_barrier_semaphore()

    @pl.loop(1, 8)
    def _(j):
        pl.semaphore_signal(barrier, inc=1, device_id=col_peer(j)[1], device_id_type=MESH)

    @pl.loop(1, 32)
    def _(j):
        pl.semaphore_signal(barrier, inc=1, device_id=grp_peer(j)[1], device_id_type=MESH)

    for partner in last_ids[1:]:
        pl.semaphore_signal(barrier, inc=1, device_id=partner, device_id_type=MESH)
    pl.semaphore_wait(barrier, 40)

    def rows_of(half):
        return pl.ds(half * HALF, HALF)

    def remote(src, dst, send, recv, device):
        return pltpu.make_async_remote_copy(
            src_ref=src, dst_ref=dst, send_sem=send, recv_sem=recv, device_id=device, device_id_type=MESH
        )

    def ring_copy(seq, way, half, hop):
        slot = (3, 1)[way] if hop == 0 else 2
        index = (seq * 2 + way) * 3 + (2 if hop else half)
        src = acts.at[seq, rows_of(half)] if hop == 0 else a_buf.at[seq, (3, 1)[way], rows_of(half)]
        return remote(src, a_buf.at[seq, slot, rows_of(half)], a_send.at[index], a_recv.at[index], z_ids[way])

    def swap_copy(seq):
        return remote(m_buf.at[seq, 0], m_buf.at[seq, 1], m_send.at[seq], m_recv.at[seq], far_id)

    sent = []

    def start(copy):
        copy.start()
        sent.append(copy)

    def ring_own(seq):
        for step in range(2):
            for way in range(2):
                start(ring_copy(seq, way, (way + step) % 2, 0))

    def ring_pass(seq):
        for way in range(2):
            ring_copy(seq, way, way, 0).wait_recv()
            start(ring_copy(seq, way, way, 1))

    def ring_near(seq, way):
        ring_copy(seq, way, 1 - way, 0).wait_recv()

    def ring_far(seq):
        for way in range(2):
            ring_copy(seq, way, way, 1).wait_recv()

    def bit_copy(index, ref, device):
        return remote(ref, ref, bit_send.at[index], bit_recv.at[index], device)

    def share_bits():
        for way in range(2):
            start(bit_copy(1 + way, bits.at[core, x], x_ids[way]))
        for way in range(2):
            bit_copy(1 + way, bits.at[core, x], x_ids[way]).wait_recv()
        start(bit_copy(3, bits.at[core, x_prev], x_ids[0]))
        bit_copy(3, bits.at[core, x_prev], x_ids[0]).wait_recv()
        start(bit_copy(4, bits.at[core], core_id))

    def sign_tables():
        bit_copy(4, bits.at[core], core_id).wait_recv()

        @pl.loop(0, 8)
        def _(i):
            row = bits[lax.rem(i, 2), 2 * y_hi + lax.div(i, 4), lax.rem(lax.div(i, 2), 2)]
            signs = (2 * row - 1).astype(jnp.float32)
            tables[i] = (walsh[...] * signs).astype(jnp.bfloat16)

    def column_signs(seq):
        signs = (2 * col_bits[...] - 1).astype(jnp.float32).astype(jnp.bfloat16)

        @pl.loop(0, TOKENS // 32)
        def _(i):
            rows = pl.ds(pl.multiple_of(i * 32, 32), 32)
            m_buf[seq, 0, rows] = m_buf[seq, 0, rows] * signs

    core_sign = (1 - 2 * core).astype(jnp.float32)

    def compute(unit, seq, slot, m):
        block = lax.rem(z + slot, 4)
        counted = mask[seq].astype(jnp.float32).astype(jnp.bfloat16)

        @pl.loop(0, 2)
        def _(b):
            columns = pl.ds(pl.multiple_of(b * 256, 256), 256)
            rows_first = a_buf[seq, slot, :, columns].T * counted
            tile = jnp.dot(rows_first, m_buf[seq, m], preferred_element_type=jnp.float32)
            coarse = tile.astype(jnp.bfloat16)
            fine = (tile - coarse.astype(jnp.float32)).astype(jnp.bfloat16)
            table = tables[2 * block + b]
            mixed = jnp.dot(table, coarse, preferred_element_type=jnp.float32)
            mixed += jnp.dot(table, fine, preferred_element_type=jnp.float32)
            part[unit, b] = mixed

        @pl.loop(0, 16)
        def _(i):
            rows = pl.ds(pl.multiple_of(i * 16, 16), 16)
            low = part[unit, 0, rows]
            high = part[unit, 1, rows] * core_sign
            part[unit, 0, rows] = low + high
            part[unit, 1, rows] = low - high

        start(core_copy(unit))

    def core_copy(unit):
        return remote(part.at[unit, 1], core_in.at[unit], core_send.at[unit], core_recv.at[unit], core_id)

    def chunk(unit, x_of):
        return part.at[unit, 0, pl.ds(pl.multiple_of(x_of * 64, 64), 64)]

    def x_half_copy(unit, way):
        rows = pl.ds(pl.multiple_of(x_far * 64 + way * 32, 32), 32)
        index = unit * 2 + way
        return remote(
            part.at[unit, 0, rows], x_half.at[unit, way], xh_send.at[index], xh_recv.at[index], x_ids[way]
        )

    def x_full_copy(unit, way):
        index = unit * 2 + way
        src = chunk(unit, (x_next, x_prev)[way])
        return remote(src, x_full.at[unit, way], xf_send.at[index], xf_recv.at[index], x_ids[way])

    def y_copy(unit):
        rows = pl.ds(pl.multiple_of(x * 64 + (1 - y_lo) * 32, 32), 32)
        return remote(part.at[unit, 0, rows], y_in.at[unit], y_send.at[unit], y_recv.at[unit], pair_id)

    def sum_core(unit):
        core_copy(unit).wait_recv()

        def add(first, rows):
            @pl.loop(0, rows // 8)
            def _(i):
                there = pl.ds(pl.multiple_of(first + i * 8, 8), 8)
                part[unit, 0, there] += core_in[unit, there]

        add(x_far * 64, 64)
        for way in range(2):
            start(x_half_copy(unit, way))
        for other in (x_next, x_prev, x):
            add(other * 64, 64)

    def sum_half(unit):
        for way in range(2):
            x_half_copy(unit, way).wait_recv()
            first = (x_next, x_prev)[way] * 64 + way * 32

            @pl.loop(0, 4)
            def _(i):
                there = pl.ds(pl.multiple_of(first + i * 8, 8), 8)
                part[unit, 0, there] += x_half[unit, way, pl.ds(pl.multiple_of(i * 8, 8), 8)]

            start(x_full_copy(unit, way))

    def sum_full(unit):
        for way in range(2):
            x_full_copy(unit, way).wait_recv()

        @pl.loop(0, 8)
        def _(i):
            there = pl.ds(pl.multiple_of(x * 64 + i * 8, 8), 8)
            here = pl.ds(pl.multiple_of(i * 8, 8), 8)
            part[unit, 0, there] += x_full[unit, 0, here] + x_full[unit, 1, here]

        start(y_copy(unit))

    def finish(unit, seq, slot, m):
        block = lax.rem(z + slot, 4)
        columns = pl.ds(pl.multiple_of(lax.rem(m + y_hi, 2) * FEATS, FEATS), FEATS)
        y_copy(unit).wait_recv()

        @pl.loop(0, 4)
        def _(i):
            here = pl.ds(pl.multiple_of(i * 8, 8), 8)
            there = pl.ds(pl.multiple_of(x * 64 + y_lo * 32 + i * 8, 8), 8)
            sums[seq, block, here, columns] = part[unit, 0, there] + y_in[unit, here]

    def piece(peer):
        return pl.ds(pl.multiple_of(peer * 32, 32), 32)

    def col_copy(seq, j):
        peer, device = col_peer(j)
        return remote(
            work.at[seq, piece(peer)], got.at[seq, col_me], col_send.at[seq, j], col_recv.at[seq, j], device
        )

    def grp_copy(seq, j):
        peer, device = grp_peer(j)
        return remote(
            ready.at[seq, peer], land.at[seq, grp_me], grp_send.at[seq, j], grp_recv.at[seq, j], device
        )

    def red_copy(j):
        return remote(mine, theirs.at[grp_me], red_send.at[j], red_recv.at[j], grp_peer(j)[1])

    last_me = y_hi * 2 + core

    def late_copy(step):
        return remote(
            late.at[4], late.at[last_me], late_send.at[step], late_recv.at[step], last_ids[step]
        )

    def pair(low, high):
        return low + high, low - high

    def four(values):
        a, b = pair(values[0], values[2])
        c, d = pair(values[1], values[3])
        first, second = pair(a, c)
        third, fourth = pair(b, d)
        return first, second, third, fourth

    def mix_local(seq):
        @pl.loop(0, 4)
        def _(q):
            rows = pl.ds(pl.multiple_of(q * 8, 8), 8)
            for half in range(2):
                columns = slice(half * 256, half * 256 + 256)
                upper = slice(512 + half * 256, 768 + half * 256)
                left = four([sums[seq, a, rows, columns] for a in range(4)])
                right = four([sums[seq, a, rows, upper] for a in range(4)])
                for a in range(4):
                    low, high = pair(left[a], right[a])
                    work[seq, pl.ds(pl.multiple_of(q * 32 + a * 8, 8), 8), columns] = low
                    work[seq, pl.ds(pl.multiple_of(128 + q * 32 + a * 8, 8), 8), columns] = high

        values = work[seq]
        coarse = values.astype(jnp.bfloat16)
        fine = (values - coarse.astype(jnp.float32)).astype(jnp.bfloat16)
        mixed = jnp.dot(coarse, wide[...], preferred_element_type=jnp.float32)
        mixed += jnp.dot(fine, wide[...], preferred_element_type=jnp.float32)
        work[seq] = mixed * (1.0 / D)

    def mix_cols(seq):
        @pl.loop(0, 4)
        def _(o):
            for part in range(2):
                columns = slice(part * 256, part * 256 + 256)
                rows = pl.ds(pl.multiple_of(o * 8, 8), 8)
                left = four([got[seq, src, rows, columns] for src in range(4)])
                right = four([got[seq, 4 + src, rows, columns] for src in range(4)])
                for c in range(4):
                    low, high = pair(left[c], right[c])
                    ready[seq, o * 4 + c, :, columns] = low
                    ready[seq, 16 + o * 4 + c, :, columns] = high

    def mix(seq):
        mix_local(seq)

        @pl.loop(1, 8)
        def _(j):
            col_copy(seq, j).start()

        got[seq, col_me] = work[seq, piece(col_me)]

    def trade(seq):
        @pl.loop(1, 8)
        def _(j):
            col_copy(seq, j).wait_recv()

        mix_cols(seq)

        @pl.loop(1, 32)
        def _(j):
            grp_copy(seq, j).start()

        land[seq, grp_me] = ready[seq, grp_me]

    lanes = lax.broadcasted_iota(jnp.int32, (1, 128), 1)

    def score_terms(seq, row):
        @pl.loop(1, 32)
        def _(j):
            grp_copy(seq, j).wait_recv()

        def add(i, carry):
            rows = pl.ds(pl.multiple_of(i * 8, 8), 8)
            value = land[seq, i]
            other = (chosen_0, chosen_1)[seq][rows]
            out[seq, rows] = value
            terms = (value * other, value * value, other * other)
            return tuple(total + term for total, term in zip(carry, terms))

        zero = tuple(jnp.zeros((8, 512), jnp.float32) for _ in range(3))
        for kind, total in enumerate(lax.fori_loop(0, 32, add, zero)):
            total = jnp.sum(jnp.sum(total, axis=1, keepdims=True), axis=0, keepdims=True)
            row = row + jnp.where(lanes == 2 * kind + seq, total, 0.0)
        return row

    ring_own(0)
    walsh[...] = hadamard_rows(0, 256, 256)
    bit_own.wait()
    start(bit_copy(0, bits.at[core, x, y_lo], pair_id))
    m_own[0].wait()
    column_signs(0)
    start(swap_copy(0))
    m_own[1].wait()
    column_signs(1)
    start(swap_copy(1))
    bit_copy(0, bits.at[core, x, y_lo], pair_id).wait_recv()
    share_bits()
    for copy in a_own:
        copy.wait()
    sign_tables()

    @pl.loop(0, 8)
    def _(i):
        rows = pl.ds(pl.multiple_of(i * 64, 64), 64)
        wide[rows] = hadamard_rows(i * 64, 64, 512).astype(jnp.bfloat16)

    row = jnp.zeros((1, 128), jnp.float32)
    here = {("a", 0, 0), ("a", 1, 0), ("m", 0, 0), ("m", 1, 0)}

    def once(key, wait):
        if key not in here:
            here.add(key)
            wait()

    for step, *rest in ORDER:
        if step == "mix":
            mix(rest[0])
            continue
        if step == "cols":
            trade(rest[0])
            continue
        if step == "land":
            row = score_terms(rest[0], row)
            continue
        if step == "rpass":
            ring_pass(rest[0])
            if rest[0] == 0:
                ring_own(1)
            continue
        seq, slot, m = rest
        unit = (seq * BLOCKS + slot) * 2 + m
        if step == "run":
            if slot == 2:
                once(("a", seq, 2), lambda seq=seq: ring_far(seq))
            else:
                once(("a", seq, slot), lambda seq=seq, slot=slot: ring_near(seq, 0 if slot == 3 else 1))
            once(("m", seq, m), lambda seq=seq: swap_copy(seq).wait_recv())
            compute(unit, seq, slot, m)
        elif step == "core":
            sum_core(unit)
        elif step == "half":
            sum_half(unit)
        elif step == "full":
            sum_full(unit)
        else:
            finish(unit, seq, slot, m)
    mine[...] = row

    @pl.loop(1, 32)
    def _(j):
        red_copy(j).start()

    theirs[grp_me] = row

    @pl.loop(1, 32)
    def _(j):
        red_copy(j).wait_recv()

    row = lax.fori_loop(0, 32, lambda i, total: total + theirs[i], jnp.zeros((1, 128), jnp.float32))
    late[4] = row
    for step in range(3):
        late_copy(step).start()
    late[last_me] = row
    for step in range(3):
        late_copy(step).wait_recv()
    totals[...] = (late[0] + late[1]) + (late[2] + late[3])

    for copy in sent:
        copy.wait_send()
    for seq in range(SEQS):

        @pl.loop(1, 8)
        def _(j):
            col_copy(seq, j).wait_send()

        @pl.loop(1, 32)
        def _(j):
            grp_copy(seq, j).wait_send()

    @pl.loop(1, 32)
    def _(j):
        red_copy(j).wait_send()

    for step in range(3):
        late_copy(step).wait_send()


def prints_and_totals(acts, grads, row_bits, col_bits, mask, chosen_0, chosen_1):
    dma = pltpu.SemaphoreType.DMA
    vmem = pl.BlockSpec(memory_space=pltpu.VMEM)
    return pl.pallas_call(
        gather_kernel,
        out_shape=(
            jax.ShapeDtypeStruct((SEQS, 256, FEATS), jnp.float32),
            jax.ShapeDtypeStruct((1, 128), jnp.float32),
        ),
        in_specs=[
            pl.BlockSpec(memory_space=pl.ANY),
            pl.BlockSpec(memory_space=pl.ANY),
            pl.BlockSpec(memory_space=pl.ANY),
            vmem,
            vmem,
            vmem,
            vmem,
        ],
        out_specs=(vmem, vmem),
        scratch_shapes=[
            pltpu.VMEM((SEQS, BLOCKS, 32, 2 * FEATS), jnp.float32),
            pltpu.VMEM((2, 4, 2, 1, 256), jnp.int32),
            pltpu.VMEM((256, 256), jnp.float32),
            pltpu.VMEM((8, 256, 256), jnp.bfloat16),
            pltpu.VMEM((SEQS, BLOCKS, TOKENS, FEATS), jnp.bfloat16),
            pltpu.VMEM((SEQS, 2, TOKENS, FEATS), jnp.bfloat16),
            pltpu.VMEM((UNITS, 2, 256, FEATS), jnp.float32),
            pltpu.VMEM((UNITS, 256, FEATS), jnp.float32),
            pltpu.VMEM((UNITS, 2, 32, FEATS), jnp.float32),
            pltpu.VMEM((UNITS, 2, 64, FEATS), jnp.float32),
            pltpu.VMEM((UNITS, 32, FEATS), jnp.float32),
            dma((4,)),
            dma((12,)),
            dma((12,)),
            dma((2,)),
            dma((2,)),
            dma((UNITS,)),
            dma((UNITS,)),
            dma((2 * UNITS,)),
            dma((2 * UNITS,)),
            dma((2 * UNITS,)),
            dma((2 * UNITS,)),
            dma((UNITS,)),
            dma((UNITS,)),
            dma,
            dma((5,)),
            dma((5,)),
            pltpu.VMEM((512, 512), jnp.bfloat16),
            pltpu.VMEM((SEQS, 256, 512), jnp.float32),
            pltpu.VMEM((SEQS, 8, 32, 512), jnp.float32),
            pltpu.VMEM((SEQS, 32, 8, 512), jnp.float32),
            pltpu.VMEM((SEQS, 32, 8, 512), jnp.float32),
            pltpu.VMEM((1, 128), jnp.float32),
            pltpu.VMEM((32, 1, 128), jnp.float32),
            pltpu.VMEM((5, 1, 128), jnp.float32),
            dma((SEQS, 8)),
            dma((SEQS, 8)),
            dma((SEQS, 32)),
            dma((SEQS, 32)),
            dma((32,)),
            dma((32,)),
            dma((3,)),
            dma((3,)),
        ],
        compiler_params=pltpu.CompilerParams(
            collective_id=0, has_side_effects=True, vmem_limit_bytes=67043328
        ),
    )(acts, grads, row_bits, col_bits, mask, chosen_0, chosen_1)


def body(activations, out_grads, token_mask, row_signs, col_signs, bank, bank_index):
    squared = float(D) * float(D)
    chosen = [
        lax.dynamic_index_in_dim(bank, bank_index[seq], 0, keepdims=False, allow_negative_indices=False)
        for seq in range(SEQS)
    ]
    prints, totals = prints_and_totals(
        activations,
        out_grads,
        row_signs.reshape(1, 256),
        col_signs.reshape(1, FEATS),
        token_mask.reshape(SEQS, 1, TOKENS),
        *chosen,
    )
    cross, own, refsq = totals[0, 0:2], totals[0, 2:4], totals[0, 4:6]
    scores = D * (cross / squared) / jnp.sqrt((own / squared + 1e-06) * (refsq / squared + 1e-06))
    return prints, scores


def solution(mesh):
    split = Mesh(mesh.devices.reshape(4, 2, 2, 2, 4), EVERY)
    return jax.shard_map(
        body,
        mesh=split,
        in_specs=(
            P(None, TOK, COL),
            P(None, TOK, COL),
            P(None, TOK),
            P(TOK),
            P(COL),
            P(None, TOK, COL),
            P(),
        ),
        out_specs=(P(None, TOK, COL), P()),
        check_vma=False,
    )
```

time: 192 us -> 214 us (1.11)
  Pallas kernels: 183 us -> 203 us
    pallas_call x2 -> x1, Pallas kernels: 183 us -> 203 us  [prints_and_totals(): pl.pallas_call(gather_kernel, out_shape=(jax.ShapeDtypeStruct((SEQS, 256,...]
where the time goes in v4:
time: 214 us; the launch traced here: 213 us
  Pallas kernels  203 us (95%)
  local copies, waits for them, and re-layouts  8.4 us (4%)
    pallas_call x1, Pallas kernels, prints_and_totals(): pl.pallas_call(gather_kernel, out_shape=(jax.ShapeDtypeStruct((SEQS, 256,...  203 us

profile of v4, /device:TPU:1, one launch (start us, length us, event | category | flops | bytes accessed | tf_op | source)
XLA Modules:
  0.0 213.4 jit_solution(12077554923124001777)
XLA Ops:
  0.6 1.3 fusion
  1.9 1.3 reshape.27.mask
  3.3 3.5 %dynamic-slice_bitcast_fusion = (f32[256,512]{1,0:T(8,128)}, f32[256,512]{1,0:T(8,128)}) fusion(f32[16,256,512]{2,1,0:T(8,128)} %param.12, s32[]{:T(128)} %bitcast.4, s32[]{:T(128)} %bitcast.2), kind=kLoop, calls=%fused_computation | loop fusion | bytes 2097160 | tf_op jit(solution)/shard_map/jit(dynamic_index_in_dim)/squeeze | solution.py:681
  6.8 203.1 %shard_map.86 = (f32[2,256,512]{2,1,0:T(8,128)}, f32[1,128]{1,0:T(1,128)}) custom-call(bf16[2,1536,512]{2,1,0:T(8,128)(2,1)} %acts.1, bf16[2,1536,512]{2,1,0:T(8,128)(2,1)} %grads.1, s32[1,256]{1,0:T(1,128)} %bitcast.11, s32[1,512]{1,0:T(1,128)} %bitcast.10, s32[2,1,1536]{2,1,0:T(1,128)} %reshape.27.mask, f32[256,512]{1,0:T(8,128)} %get-tuple-element.7.chosen_0, ...), custom_call_target="tpu_custom_call" | custom-call | tf_op jit(solution)/shard_map/pallas_call | solution.py:611
  209.9 1.3 multiply_bitcast_fusion
  211.1 2.3 %copy.10 = f32[2,256,512]{2,1,0:T(8,128)} copy(f32[2,256,512]{2,1,0:T(8,128)} %get-tuple-element.12) | data formatting | bytes 2097152

commit v5 on v3

--- a/solution.py
+++ b/solution.py
@@ -272,7 +272,7 @@
 
     def compute(unit, seq, slot, m):
         block = lax.rem(z + slot, 4)
-        counted = mask[seq].astype(jnp.float32).astype(jnp.bfloat16)
+        counted = mask[seq : seq + 1, :].astype(jnp.float32).astype(jnp.bfloat16)
 
         @pl.loop(0, 2)
         def _(b):
@@ -484,7 +484,6 @@
     mine,
     theirs,
     late,
-    late_in,
     col_send,
     col_recv,
     grp_send,
@@ -515,6 +514,8 @@
 
     core_id = (x, y_lo, 1 - core, y_hi, z)
     far_id = (x, y_lo, core, 1 - y_hi, z)
+    last_ids = (far_id, core_id, (x, y_lo, 1 - core, 1 - y_hi, z))
+    last_me = y_hi * 2 + core
 
     barrier = pltpu.get_barrier_semaphore()
 
@@ -526,7 +527,8 @@
     def _(j):
         pl.semaphore_signal(barrier, inc=1, device_id=grp_peer(j)[1], device_id_type=MESH)
 
-    pl.semaphore_signal(barrier, inc=1, device_id=core_id, device_id_type=MESH)
+    for partner in last_ids[1:]:
+        pl.semaphore_signal(barrier, inc=1, device_id=partner, device_id_type=MESH)
 
     @pl.loop(0, 8)
     def _(i):
@@ -557,9 +559,7 @@
         return remote(mine, theirs.at[grp_me], red_send.at[j], red_recv.at[j], grp_peer(j)[1])
 
     def late_copy(step):
-        return remote(
-            late.at[step], late_in.at[step], late_send.at[step], late_recv.at[step], (far_id, core_id)[step]
-        )
+        return remote(late.at[4], late.at[last_me], late_send.at[step], late_recv.at[step], last_ids[step])
 
     def pair(low, high):
         return low + high, low - high
@@ -608,7 +608,7 @@
     for seq in range(SEQS):
         mix_local(seq)
         if seq == 0:
-            pl.semaphore_wait(barrier, 39)
+            pl.semaphore_wait(barrier, 40)
 
         @pl.loop(1, 8)
         def _(j):
@@ -630,7 +630,8 @@
 
         land[seq, grp_me] = ready[seq, grp_me]
 
-    mine[...] = jnp.zeros((8, 128), jnp.float32)
+    lanes = lax.broadcasted_iota(jnp.int32, (1, 128), 1)
+    row = jnp.zeros((1, 128), jnp.float32)
     for seq in range(SEQS):
 
         @pl.loop(1, 32)
@@ -647,27 +648,29 @@
 
         start = tuple(jnp.zeros((8, 512), jnp.float32) for _ in range(3))
         for kind, total in enumerate(lax.fori_loop(0, 32, add, start)):
-            total = total[:, 0:128] + total[:, 128:256] + total[:, 256:384] + total[:, 384:512]
-            mine[2 * kind + seq : 2 * kind + seq + 1, :] = jnp.sum(total, axis=0, keepdims=True)
+            total = jnp.sum(jnp.sum(total, axis=1, keepdims=True), axis=0, keepdims=True)
+            row = row + jnp.where(lanes == 2 * kind + seq, total, 0.0)
+
+    mine[...] = row
 
     @pl.loop(1, 32)
     def _(j):
         red_copy(j).start()
 
-    theirs[grp_me] = mine[...]
+    theirs[grp_me] = row
 
     @pl.loop(1, 32)
     def _(j):
         red_copy(j).wait_recv()
 
-    late[0] = lax.fori_loop(0, 32, lambda i, total: total + theirs[i], jnp.zeros((8, 128), jnp.float32))
-    for step in range(2):
+    row = lax.fori_loop(0, 32, lambda i, total: total + theirs[i], jnp.zeros((1, 128), jnp.float32))
+    late[4] = row
+    for step in range(3):
         late_copy(step).start()
+    late[last_me] = row
+    for step in range(3):
         late_copy(step).wait_recv()
-        both = late[step] + late_in[step]
-        if step == 0:
-            late[1] = both
-    totals[...] = jnp.broadcast_to(jnp.sum(both, axis=1, keepdims=True), (8, 128))
+    totals[...] = (late[0] + late[1]) + (late[2] + late[3])
 
     for seq in range(SEQS):
 
@@ -683,7 +686,7 @@
     def _(j):
         red_copy(j).wait_send()
 
-    for step in range(2):
+    for step in range(3):
         late_copy(step).wait_send()
 
 
@@ -694,7 +697,7 @@
         mix_kernel,
         out_shape=(
             jax.ShapeDtypeStruct((SEQS, 256, 512), jnp.float32),
-            jax.ShapeDtypeStruct((8, 128), jnp.float32),
+            jax.ShapeDtypeStruct((1, 128), jnp.float32),
         ),
         in_specs=[vmem, vmem, vmem],
         out_specs=(vmem, vmem),
@@ -704,18 +707,17 @@
             pltpu.VMEM((SEQS, 8, 32, 512), jnp.float32),
             pltpu.VMEM((SEQS, 32, 8, 512), jnp.float32),
             pltpu.VMEM((SEQS, 32, 8, 512), jnp.float32),
-            pltpu.VMEM((8, 128), jnp.float32),
-            pltpu.VMEM((32, 8, 128), jnp.float32),
-            pltpu.VMEM((2, 8, 128), jnp.float32),
-            pltpu.VMEM((2, 8, 128), jnp.float32),
+            pltpu.VMEM((1, 128), jnp.float32),
+            pltpu.VMEM((32, 1, 128), jnp.float32),
+            pltpu.VMEM((5, 1, 128), jnp.float32),
             dma((SEQS, 8)),
             dma((SEQS, 8)),
             dma((SEQS, 32)),
             dma((SEQS, 32)),
             dma((32,)),
             dma((32,)),
-            dma((2,)),
-            dma((2,)),
+            dma((3,)),
+            dma((3,)),
         ],
         compiler_params=pltpu.CompilerParams(
             collective_id=1, has_side_effects=True, vmem_limit_bytes=32 * 1024 * 1024
@@ -730,14 +732,14 @@
         out_grads,
         row_signs.reshape(1, 256),
         col_signs.reshape(1, FEATS),
-        token_mask.reshape(SEQS, 1, TOKENS),
+        token_mask,
     )
     chosen = [
         lax.dynamic_index_in_dim(bank, bank_index[seq], 0, keepdims=False, allow_negative_indices=False)
         for seq in range(SEQS)
     ]
     prints, totals = mixed_prints(sums, *chosen)
-    cross, own, refsq = totals[0:2, 0], totals[2:4, 0], totals[4:6, 0]
+    cross, own, refsq = totals[0, 0:2], totals[0, 2:4], totals[0, 4:6]
     scores = D * (cross / squared) / jnp.sqrt((own / squared + 1e-06) * (refsq / squared + 1e-06))
     return prints, scores
 

time: 192 us -> 192 us (level)
  Pallas kernels: 183 us -> 181 us
    pallas_call x1, Pallas kernels: 48.2 us -> 46.1 us  [mixed_prints(): pl.pallas_call(mix_kernel, out_shape=(jax.ShapeDtypeStruct((SEQS, 256, 51...]
    unnamed x3 -> x7, local copies, waits for them, and re-layouts: 2.19 us -> 4.27 us
where the time goes in v5:
time: 192 us; the launch traced here: 191 us
  Pallas kernels  181 us (94%)
  local copies, waits for them, and re-layouts  9.04 us (5%)
    pallas_call x1, Pallas kernels, gathered_products(): pl.pallas_call(gather_kernel, out_shape=jax.ShapeDtypeStruct((SEQS, BLOCK...  135 us
    pallas_call x1, Pallas kernels, mixed_prints(): pl.pallas_call(mix_kernel, out_shape=(jax.ShapeDtypeStruct((SEQS, 256, 51...  46.1 us
    unnamed x7, local copies, waits for them, and re-layouts  4.27 us

profile of v5, /device:TPU:1, one launch (start us, length us, event | category | flops | bytes accessed | tf_op | source)
XLA Modules:
  0.0 191.2 jit_solution(9614714625128759565)
XLA Ops:
  0.6 1.3 fusion
  1.9 3.5 %dynamic-slice_bitcast_fusion = (f32[256,512]{1,0:T(8,128)}, f32[256,512]{1,0:T(8,128)}) fusion(f32[16,256,512]{2,1,0:T(8,128)} %param.12, s32[]{:T(128)} %bitcast.4, s32[]{:T(128)} %bitcast.2), kind=kLoop, calls=%fused_computation | loop fusion | bytes 2097160 | tf_op jit(solution)/shard_map/jit(dynamic_index_in_dim)/squeeze | solution.py:738
  5.4 134.9 %shard_map.86.sums = f32[2,4,32,1024]{3,2,1,0:T(8,128)} custom-call(bf16[2,1536,512]{2,1,0:T(8,128)(2,1)} %acts.1, bf16[2,1536,512]{2,1,0:T(8,128)(2,1)} %grads.1, s32[1,256]{1,0:T(1,128)} %bitcast.11, s32[1,512]{1,0:T(1,128)} %bitcast.10, s32[2,1536]{1,0:T(2,128)} %mask.1), custom_call_target="tpu_custom_call" | custom-call | tf_op jit(solution)/shard_map/pallas_call | solution.py:427
  140.3 0.0 copy-start
  140.3 1.2 copy-done
  141.5 0.0 copy-start.1
  141.5 1.0 copy-done.1
  142.6 0.0 copy-start.2
  142.6 1.0 copy-done.2
  143.6 46.1 %shard_map.87 = (f32[2,256,512]{2,1,0:T(8,128)S(1)}, f32[1,128]{1,0:T(1,128)S(1)}) custom-call(f32[2,4,32,1024]{3,2,1,0:T(8,128)S(1)} %copy-done, f32[256,512]{1,0:T(8,128)S(1)} %copy-done.2, f32[256,512]{1,0:T(8,128)S(1)} %copy-done.1), custom_call_target="tpu_custom_call" | custom-call | tf_op jit(solution)/shard_map/pallas_call | solution.py:696
  189.7 0.6 multiply_bitcast_fusion
  190.3 1.0 copy.10
Async XLA Ops:
  140.3 1.2 copy-start
  141.5 1.0 copy-start.1
  142.6 1.0 copy-start.2

commit v6 on v5

--- a/solution.py
+++ b/solution.py
@@ -471,11 +471,13 @@
 
 
 def mix_kernel(
-    sums,
-    chosen_0,
-    chosen_1,
+    sums_there,
+    bank_there,
+    index,
     out,
     totals,
+    sums,
+    bank,
     walsh,
     work,
     got,
@@ -492,6 +494,7 @@
     red_recv,
     late_send,
     late_recv,
+    load_sem,
 ):
     x = lax.axis_index("tok_0")
     y_lo = lax.axis_index("tok_1")
@@ -517,6 +520,10 @@
     last_ids = (far_id, core_id, (x, y_lo, 1 - core, 1 - y_hi, z))
     last_me = y_hi * 2 + core
 
+    sums_load = pltpu.make_async_copy(sums_there, sums, load_sem.at[0])
+    bank_load = pltpu.make_async_copy(bank_there, bank, load_sem.at[1])
+    sums_load.start()
+    bank_load.start()
     barrier = pltpu.get_barrier_semaphore()
 
     @pl.loop(1, 8)
@@ -605,6 +612,7 @@
                     ready[seq, o * 4 + c, :, columns] = low
                     ready[seq, 16 + o * 4 + c, :, columns] = high
 
+    sums_load.wait()
     for seq in range(SEQS):
         mix_local(seq)
         if seq == 0:
@@ -630,6 +638,7 @@
 
         land[seq, grp_me] = ready[seq, grp_me]
 
+    bank_load.wait()
     lanes = lax.broadcasted_iota(jnp.int32, (1, 128), 1)
     row = jnp.zeros((1, 128), jnp.float32)
     for seq in range(SEQS):
@@ -638,10 +647,12 @@
         def _(j):
             grp_copy(seq, j).wait_recv()
 
+        chosen = index[seq]
+
         def add(i, carry):
             rows = pl.ds(pl.multiple_of(i * 8, 8), 8)
             value = land[seq, i]
-            other = (chosen_0, chosen_1)[seq][rows]
+            other = bank[chosen, rows]
             out[seq, rows] = value
             terms = (value * other, value * value, other * other)
             return tuple(total + term for total, term in zip(carry, terms))
@@ -690,7 +701,7 @@
         late_copy(step).wait_send()
 
 
-def mixed_prints(sums, chosen_0, chosen_1):
+def mixed_prints(sums, bank, bank_index):
     dma = pltpu.SemaphoreType.DMA
     vmem = pl.BlockSpec(memory_space=pltpu.VMEM)
     return pl.pallas_call(
@@ -699,9 +710,15 @@
             jax.ShapeDtypeStruct((SEQS, 256, 512), jnp.float32),
             jax.ShapeDtypeStruct((1, 128), jnp.float32),
         ),
-        in_specs=[vmem, vmem, vmem],
+        in_specs=[
+            pl.BlockSpec(memory_space=pl.ANY),
+            pl.BlockSpec(memory_space=pl.ANY),
+            pl.BlockSpec(memory_space=pltpu.SMEM),
+        ],
         out_specs=(vmem, vmem),
         scratch_shapes=[
+            pltpu.VMEM((SEQS, BLOCKS, 32, 2 * FEATS), jnp.float32),
+            pltpu.VMEM((16, 256, 512), jnp.float32),
             pltpu.VMEM((512, 512), jnp.bfloat16),
             pltpu.VMEM((SEQS, 256, 512), jnp.float32),
             pltpu.VMEM((SEQS, 8, 32, 512), jnp.float32),
@@ -718,11 +735,12 @@
             dma((32,)),
             dma((3,)),
             dma((3,)),
+            dma((2,)),
         ],
         compiler_params=pltpu.CompilerParams(
-            collective_id=1, has_side_effects=True, vmem_limit_bytes=32 * 1024 * 1024
+            collective_id=1, has_side_effects=True, vmem_limit_bytes=67043328
         ),
-    )(sums, chosen_0, chosen_1)
+    )(sums, bank, bank_index)
 
 
 def body(activations, out_grads, token_mask, row_signs, col_signs, bank, bank_index):
@@ -734,11 +752,7 @@
         col_signs.reshape(1, FEATS),
         token_mask,
     )
-    chosen = [
-        lax.dynamic_index_in_dim(bank, bank_index[seq], 0, keepdims=False, allow_negative_indices=False)
-        for seq in range(SEQS)
-    ]
-    prints, totals = mixed_prints(sums, *chosen)
+    prints, totals = mixed_prints(sums, bank, bank_index)
     cross, own, refsq = totals[0, 0:2], totals[0, 2:4], totals[0, 4:6]
     scores = D * (cross / squared) / jnp.sqrt((own / squared + 1e-06) * (refsq / squared + 1e-06))
     return prints, scores

time: 192 us -> 187 us (0.974)
  local copies, waits for them, and re-layouts: 9.04 us -> 2.26 us
  Pallas kernels: 181 us -> 183 us
    squeeze x1 -> x0, local copies, waits for them, and re-layouts: 3.45 us -> none  [body(): lax.dynamic_index_in_dim(bank, bank_index[seq], 0, keepdims=False, allow_...]
    unnamed x7 -> x1, local copies, waits for them, and re-layouts: 4.27 us -> 2.26 us
    pallas_call x1, Pallas kernels: 46.1 us -> 48 us  [mixed_prints(): pl.pallas_call(mix_kernel, out_shape=(jax.ShapeDtypeStruct((SEQS, 256, 51...]
where the time goes in v6:
time: 187 us
  Pallas kernels  183 us (98%)
  local copies, waits for them, and re-layouts  2.26 us (1%)
    pallas_call x1, Pallas kernels, gathered_products(): pl.pallas_call(gather_kernel, out_shape=jax.ShapeDtypeStruct((SEQS, BLOCK...  135 us
    pallas_call x1, Pallas kernels, mixed_prints(): pl.pallas_call(mix_kernel, out_shape=(jax.ShapeDtypeStruct((SEQS, 256, 51...  48 us

profile of v6, /device:TPU:1, one launch (start us, length us, event | category | flops | bytes accessed | tf_op | source)
XLA Modules:
  0.0 187.2 jit_solution(4562380663128953933)
XLA Ops:
  0.6 134.9 %shard_map.86.sums_there = f32[2,4,32,1024]{3,2,1,0:T(8,128)} custom-call(bf16[2,1536,512]{2,1,0:T(8,128)(2,1)} %acts.1, bf16[2,1536,512]{2,1,0:T(8,128)(2,1)} %grads.1, s32[1,256]{1,0:T(1,128)} %bitcast.5, s32[1,512]{1,0:T(1,128)} %bitcast.4, s32[2,1536]{1,0:T(2,128)} %mask.1), custom_call_target="tpu_custom_call" | custom-call | tf_op jit(solution)/shard_map/pallas_call | solution.py:427
  135.6 48.0 %shard_map.87 = (f32[2,256,512]{2,1,0:T(8,128)}, f32[1,128]{1,0:T(1,128)}) custom-call(f32[2,4,32,1024]{3,2,1,0:T(8,128)} %shard_map.86.sums_there, f32[16,256,512]{2,1,0:T(8,128)} %bank_there.1, s32[2]{0:T(128)} %index.1), custom_call_target="tpu_custom_call" | custom-call | tf_op jit(solution)/shard_map/pallas_call | solution.py:707
  183.6 1.3 multiply_bitcast_fusion
  185.0 2.3 %copy.10 = f32[2,256,512]{2,1,0:T(8,128)} copy(f32[2,256,512]{2,1,0:T(8,128)} %get-tuple-element.8) | data formatting | bytes 2097152

commit v7 on v6

--- a/solution.py
+++ b/solution.py
@@ -52,16 +52,16 @@
     ('full', 0, 0, 1),
     ('run', 0, 2, 1),
     ('half', 0, 1, 0),
+    ('half', 0, 1, 1),
     ('core', 0, 2, 0),
-    ('half', 0, 1, 1),
     ('end', 0, 0, 0),
     ('end', 1, 0, 0),
+    ('core', 0, 2, 1),
     ('end', 0, 3, 0),
-    ('core', 0, 2, 1),
     ('full', 0, 3, 1),
     ('full', 0, 1, 0),
+    ('full', 0, 1, 1),
     ('half', 0, 2, 0),
-    ('full', 0, 1, 1),
     ('half', 0, 2, 1),
     ('rpass', 1),
     ('full', 0, 2, 0),
@@ -90,16 +90,16 @@
     ('full', 1, 3, 0),
     ('half', 1, 1, 0),
     ('run', 1, 2, 0),
+    ('full', 1, 3, 1),
     ('run', 1, 2, 1),
-    ('full', 1, 3, 1),
     ('half', 1, 1, 1),
     ('core', 1, 2, 0),
     ('end', 1, 3, 0),
-    ('core', 1, 2, 1),
     ('full', 1, 1, 0),
     ('end', 1, 3, 1),
+    ('core', 1, 2, 1),
+    ('end', 1, 1, 0),
     ('full', 1, 1, 1),
-    ('end', 1, 1, 0),
     ('half', 1, 2, 0),
     ('half', 1, 2, 1),
     ('end', 1, 1, 1),

time: 187 us -> 187 us (level)
  no operation moved by 1% of the time
where the time goes in v7:
time: 187 us
  Pallas kernels  182 us (97%)
  local copies, waits for them, and re-layouts  2.26 us (1%)
    pallas_call x1, Pallas kernels, gathered_products(): pl.pallas_call(gather_kernel, out_shape=jax.ShapeDtypeStruct((SEQS, BLOCK...  134 us
    pallas_call x1, Pallas kernels, mixed_prints(): pl.pallas_call(mix_kernel, out_shape=(jax.ShapeDtypeStruct((SEQS, 256, 51...  48.1 us

profile of v7, /device:TPU:1, one launch (start us, length us, event | category | flops | bytes accessed | tf_op | source)
XLA Modules:
  0.0 186.7 jit_solution(1869874292468006310)
XLA Ops:
  0.6 134.4 %shard_map.86.sums_there = f32[2,4,32,1024]{3,2,1,0:T(8,128)} custom-call(bf16[2,1536,512]{2,1,0:T(8,128)(2,1)} %acts.1, bf16[2,1536,512]{2,1,0:T(8,128)(2,1)} %grads.1, s32[1,256]{1,0:T(1,128)} %bitcast.5, s32[1,512]{1,0:T(1,128)} %bitcast.4, s32[2,1536]{1,0:T(2,128)} %mask.1), custom_call_target="tpu_custom_call" | custom-call | tf_op jit(solution)/shard_map/pallas_call | solution.py:427
  135.0 48.1 %shard_map.87 = (f32[2,256,512]{2,1,0:T(8,128)}, f32[1,128]{1,0:T(1,128)}) custom-call(f32[2,4,32,1024]{3,2,1,0:T(8,128)} %shard_map.86.sums_there, f32[16,256,512]{2,1,0:T(8,128)} %bank_there.1, s32[2]{0:T(128)} %index.1), custom_call_target="tpu_custom_call" | custom-call | tf_op jit(solution)/shard_map/pallas_call | solution.py:707
  183.1 1.3 multiply_bitcast_fusion
  184.5 2.3 %copy.10 = f32[2,256,512]{2,1,0:T(8,128)} copy(f32[2,256,512]{2,1,0:T(8,128)} %get-tuple-element.8) | data formatting | bytes 2097152
